TPU v7x, 512 devices: a whole 4x8x8 slice. The times are simulated.
512 devices in a mesh: slab: 128 (over y, z, core), walk: 4 (over x).
Axes of the slice: x: 4, y: 8, z: 8, core: 2. Of those that a mesh axis runs over, the one named last changes fastest.
Arguments:
- bias_grid: float32 [512, 512, 512], P('slab', 'walk'), may hold values from 0 to 12, as said below
- hill_slab: int32 [1024, 64, 1], P(('slab', 'walk')), may hold values from 0 to 127; in each aligned block of 128 rows (0 to 127, 128 to 255, ..., all dimensions but the last counted through in order) at most 4 rows name the same one
- hill_row: int32 [1024, 64], P(('slab', 'walk')), may hold values from 0 to 3
- hill_col: int32 [1024, 64], P(('slab', 'walk')), may hold values from 0 to 511
- hill_depth: int32 [1024, 64], P(('slab', 'walk')), may hold values from 0 to 511
- hill_level: int32 [1024, 64], P(('slab', 'walk')), may hold values from 0 to 7
- hill_count: int32 [1024], P(('slab', 'walk')), may hold values from 1 to 64
- height_levels: float32 [8], replicated, may hold values from 0.5 to 2
Outputs:
- new_bias: float32 [512, 512, 512], P('slab', 'walk')
- free_energy: float32 [512, 512, 512], P('slab', 'walk')
Inputs may be any that keep to these rules, and one draw needn't show every extreme that they name: `bias_grid`: the bias is not negative. `hill_slab`: among the hills of one device's walkers (128 hills in a row of the flattened walkers and hills), no slab is named more than 4 times, and in some such blocks one slab is named exactly 4 times.
All inputs are finite; a program needn't handle non-finite values.
Results may differ from a plain program's by a relative error of at most 0.000082.
Values sent between devices are 32-bit elements; how exact they have to be, the bound alone decides.
No kernel may reach another device: no remote copies, remote signals or barrier semaphores. Data moves between devices by JAX's collectives and lax.ppermute only.
A program may use at most 64 MiB of HBM per device.

v0:
```python
import math

import jax
import jax.numpy as jnp
from jax import lax
from jax.sharding import Mesh
from jax.sharding import PartitionSpec as P

SLAB = ("slab_0", "slab_1", "slab_2")
SLAB_WALK = ("slab_0", "slab_1", "slab_2", "walk")


BASE_HEIGHT = 1.2
TEMPER = 4.0
SIGMA_SHARE = 0.3125
FREE_SCALE = 10.0 / 9.0


def laid_out(parts, dim):
    parts = jnp.moveaxis(parts, 0, dim)
    lengths = parts.shape
    return parts.reshape(*lengths[:dim], lengths[dim] * lengths[dim + 1], *lengths[dim + 2 :])


def copy_for_each(array, axis):
    peers = lax.axis_size(axis)
    return lax.all_to_all(
        jnp.broadcast_to(array[None], (peers, *array.shape)), axis, 0, 0, tiled=True
    )


def gathered_copies(array, axis, dim):
    return laid_out(copy_for_each(array, axis), dim)


def of_everyone(array, axis):
    return copy_for_each(array, axis).sum(axis=0)


def from_behind(block, axis, distance):
    devices = range(lax.axis_size(axis))
    route = [((i - distance) % len(devices), i) for i in devices]
    return lax.ppermute(block, axis, route)


def by_axis(array, axes):
    for axis in axes:
        array = lax.pmax(array, axis)
    return array


def gaussian(position, centre, extent, radius):
    offset = jnp.mod(position - centre + extent // 2, extent) - extent // 2
    inside = (offset >= -radius) & (offset < radius)
    spread = SIGMA_SHARE * radius
    distance = offset.astype(jnp.float32)
    return jnp.where(inside, jnp.exp(-(distance * distance) / (2.0 * spread * spread)), 0.0)


def deposit(row_ids, col_ids, depth_ids, hill_lists, grid_rows, grid_cols, grid_depth, radius):
    slot_total = hill_lists.shape[1]
    block_size = math.gcd(slot_total, 256)
    row_count = row_ids.shape[0]
    col_count = col_ids.shape[0]
    depth_count = depth_ids.shape[0]

    def one_block(carry_sum, index):
        portion = lax.dynamic_slice_in_dim(hill_lists, index * block_size, block_size, 1)
        row_gauss = (
            gaussian(row_ids[:, None], portion[1].astype(jnp.int32)[None, :], grid_rows, radius)
            * portion[0][None, :]
        )
        col_gauss = gaussian(
            col_ids[:, None], portion[2].astype(jnp.int32)[None, :], grid_cols, radius
        )
        depth_gauss = gaussian(
            depth_ids[None, :], portion[3].astype(jnp.int32)[:, None], grid_depth, radius
        )
        plane_gauss = (row_gauss[:, None, :] * col_gauss[None, :, :]).reshape(
            row_count * col_count, block_size
        )
        added = jnp.dot(
            plane_gauss,
            depth_gauss,
            precision=lax.Precision.HIGHEST,
            preferred_element_type=jnp.float32,
        )
        return (carry_sum + added, None)

    start = jnp.zeros((row_count * col_count, depth_count), jnp.float32)
    result, unused = lax.scan(one_block, start, jnp.arange(slot_total // block_size))
    return result.reshape(row_count, col_count, depth_count)


def per_device(
    bias_grid, hill_slab, hill_row, hill_col, hill_depth, hill_level, hill_count, height_levels
):
    rows_dev, cols_dev, depth_bins = bias_grid.shape
    slab_count = lax.axis_size(SLAB)
    walk_count = lax.axis_size("walk")
    radius = 2 * rows_dev
    grid_rows = rows_dev * slab_count
    grid_cols = cols_dev * walk_count
    walkers_dev, hill_slots = hill_row.shape
    sent_rows = walkers_dev * hill_slots
    capacity = max(2, 4 * sent_rows // slab_count)
    target = hill_slab[:, :, 0].reshape(-1)
    centre_row = target * rows_dev + hill_row.reshape(-1)
    is_live = (
        lax.broadcasted_iota(jnp.int32, (walkers_dev, hill_slots), 1) < hill_count[:, None]
    ).reshape(-1)
    level_match = hill_level.reshape(-1)[:, None] == lax.broadcasted_iota(
        jnp.int32, (1, height_levels.shape[0]), 1
    )
    base_height = jnp.sum(jnp.where(level_match, height_levels[None, :], 0.0), axis=1)
    base_height = jnp.where(is_live, BASE_HEIGHT * base_height, 0.0)
    same_slab = target[:, None] == target[None, :]
    earlier = lax.broadcasted_iota(jnp.int32, (sent_rows, sent_rows), 1) < lax.broadcasted_iota(
        jnp.int32, (sent_rows, sent_rows), 0
    )
    slot_rank = jnp.sum((same_slab & earlier).astype(jnp.int32), axis=1)
    slot_place = target * capacity + slot_rank
    placing = (
        slot_place[:, None] == lax.broadcasted_iota(jnp.int32, (1, slab_count * capacity), 1)
    ).astype(jnp.float32)
    fields = jnp.stack(
        [
            base_height,
            centre_row.astype(jnp.float32),
            hill_col.reshape(-1).astype(jnp.float32),
            hill_depth.reshape(-1).astype(jnp.float32),
        ]
    )
    outgoing = jnp.dot(
        fields, placing, precision=lax.Precision.HIGHEST, preferred_element_type=jnp.float32
    )
    outgoing = outgoing.reshape(4, slab_count, capacity)
    arrived = lax.all_to_all(outgoing, SLAB, split_axis=1, concat_axis=1, tiled=True).reshape(
        4, slab_count * capacity
    )
    shared = gathered_copies(arrived, "walk", 1)
    slab_index = lax.axis_index(SLAB)
    walk_index = lax.axis_index("walk")
    local_row = jnp.clip(shared[1].astype(jnp.int32) - slab_index * rows_dev, 0, rows_dev - 1)
    local_col = shared[2].astype(jnp.int32) - walk_index * cols_dev
    local_depth = jnp.clip(shared[3].astype(jnp.int32), 0, depth_bins - 1)
    owned = (local_col >= 0) & (local_col < cols_dev)
    flat_place = (
        local_row * cols_dev + jnp.clip(local_col, 0, cols_dev - 1)
    ) * depth_bins + local_depth
    picked = bias_grid.reshape(-1)[flat_place]
    centre_value = of_everyone(jnp.where(owned, picked, 0.0), "walk")
    height = shared[0] * jnp.exp(-centre_value / TEMPER)
    hill_lists = jnp.stack([height, shared[1], shared[2], shared[3]])
    col_ids = walk_index * cols_dev + lax.broadcasted_iota(jnp.int32, (cols_dev,), 0)
    depth_ids = lax.broadcasted_iota(jnp.int32, (depth_bins,), 0)
    row_ids = (
        slab_index * rows_dev
        - radius
        + lax.broadcasted_iota(jnp.int32, (rows_dev + 2 * radius,), 0)
    )
    padded = deposit(
        row_ids, col_ids, depth_ids, hill_lists, grid_rows, grid_cols, depth_bins, radius
    )
    added = padded[radius : radius + rows_dev]
    for block in (0, 1, 3, 4):
        rim_part = padded[block * rows_dev : (block + 1) * rows_dev]
        added = added + from_behind(rim_part, SLAB, block - 2)
    new_bias = bias_grid + added
    highest = by_axis(jnp.max(new_bias), SLAB_WALK)
    free_energy = FREE_SCALE * (highest - new_bias)
    return (new_bias, free_energy)


def solution(mesh):
    split = Mesh(
        mesh.devices.reshape(8, 8, 2, mesh.shape["walk"]), ("slab_0", "slab_1", "slab_2", "walk")
    )
    in_specs = (
        P(SLAB, "walk", None),
        P(SLAB_WALK, None, None),
        P(SLAB_WALK, None),
        P(SLAB_WALK, None),
        P(SLAB_WALK, None),
        P(SLAB_WALK, None),
        P(SLAB_WALK),
        P(),
    )
    out_specs = (P(SLAB, "walk", None), P(SLAB, "walk", None))
    return jax.shard_map(
        per_device, mesh=split, in_specs=in_specs, out_specs=out_specs, check_vma=False
    )
```

profile of v0, /device:TPU:1, one launch (start us, length us, event | category | flops | bytes accessed | tf_op | source)
XLA Modules:
  0.0 253.1 jit_solution(1350240371032269089)
XLA Ops:
  0.6 0.8 reshape.397
  1.4 0.8 eq.49
  2.1 0.7 iota_compare_fusion.4
  3.0 0.7 convert_element_type.140
  3.7 0.7 convert_element_type.142
  4.5 0.5 broadcast.592
  5.0 1.3 multiply_reduce_fusion
  6.5 0.2 convert_reduce_fusion
  6.7 0.7 select_reduce_fusion
  7.5 0.3 fusion.45
  7.7 0.3 reshape.398
  8.0 0.2 copy.19
  8.2 32.5 %all_to_all.16 = f32[4,128,4]{2,0,1:T(4,128)S(1)} all-to-all(f32[4,128,4]{2,0,1:T(4,128)S(1)} %copy.19), channel_id=1, replica_groups=mesh['slab_0'=8,'slab_1'=8,'slab_2'=2,'walk'=4] {'slab_0','slab_1','slab..., dimensions={1} | all-to-all | bytes 16384 | tf_op jit(solution)/shard_map/all_to_all | solution.py:138
  40.9 0.6 broadcast_in_dim.69
  41.5 4.0 %all-to-all-start.1 = ((f32[4,4,512]{2,1,0:T(4,128)}), f32[4,4,512]{2,1,0:T(4,128)S(1)}, u32[]{:S(2)}, u32[]{:S(2)}) async-start(f32[4,4,512]{2,1,0:T(4,128)} %broadcast_in_dim.69), calls=%async_computation.1 | async-start | bytes 65536 | tf_op jit(solution)/shard_map/all_to_all | solution.py:27
  45.5 1.5 copy.26
  47.0 2.8 %all-to-all-done.1 = f32[4,4,512]{2,1,0:T(4,128)S(1)} async-done(((f32[4,4,512]{2,1,0:T(4,128)}), f32[4,4,512]{2,1,0:T(4,128)S(1)}, u32[]{:S(2)}, u32[]{:S(2)}) %all-to-all-start.1) | async-done | bytes 32800 | tf_op jit(solution)/shard_map/all_to_all | solution.py:27
  49.9 11.8 %gather_fusion = f32[2048]{0:T(1024)S(1)} fusion(f32[262144]{0:T(1024)S(1)} %bitcast.56, s32[2048]{0:T(1024)S(1)} %broadcast_clamp_fusion), kind=kCustom, calls=%fused_computation | custom fusion | bytes 24576 | tf_op jit(solution)/shard_map/gather | solution.py:151
  61.8 0.6 broadcast_in_dim.71
  62.4 3.3 %all-to-all-start.2 = ((f32[4,1,2048]{2,1,0:T(1,128)}), f32[4,1,2048]{2,1,0:T(1,128)S(1)}, u32[]{:S(2)}, u32[]{:S(2)}) async-start(f32[4,1,2048]{2,1,0:T(1,128)} %broadcast_in_dim.71), calls=%async_computation.2 | async-start | bytes 65536 | tf_op jit(solution)/shard_map/all_to_all | solution.py:27
  65.7 4.2 %all-to-all-done.2 = f32[4,1,2048]{2,1,0:T(1,128)S(1)} async-done(((f32[4,1,2048]{2,1,0:T(1,128)}), f32[4,1,2048]{2,1,0:T(1,128)S(1)}, u32[]{:S(2)}, u32[]{:S(2)}) %all-to-all-start.2) | async-done | bytes 32800 | tf_op jit(solution)/shard_map/all_to_all | solution.py:27
  70.0 85.6 %while.14 = (s32[]{:T(128)}, f32[2560,512]{1,0:T(8,128)}, s32[8]{0:T(128)S(1)}, f32[4,2048]{1,0:T(4,128)S(1)}, s32[]{:T(128)}, /*index=5*/s32[]{:T(128)}, s32[]{...) while((s32[]{:T(128)}, f32[2560,512]{1,0:T(8,128)}, s32[8]{0:T(128)S(1)}, ...), condition=%wide.region_4.5_spmd.clone, body=%wide.region_3.4_spmd.clone.sunk | while | flops 4033531904 | bytes 16045477 | solution.py:91
  70.1 0.6 dynamic_slice.18
  71.5 0.2 exponential_select_fusion.2
  71.7 0.3 broadcast_multiply_fusion.2
  72.0 7.3 %select_add_fusion.2 = f32[2560,512]{1,0:T(8,128)} fusion(f32[2560,512]{1,0:T(8,128)} %get-tuple-element.236, f32[2560,256]{1,0:T(8,128)S(1)} %bitcast.55, pred[]{:T(512)S(6)} %compare.9, s32[256]{0:T(256)S(1)} %bitcast.69), kind=kOutput, calls=%fused_computation.4.clone.1 | convolution fusion | flops 4032036864 | bytes 13108225 | tf_op jit(solution)/shard_map/while/body/eval_jaxpr/dot_general | solution.py:82
  79.3 0.6 dynamic_slice.18
  80.7 0.2 exponential_select_fusion.2
  80.9 0.3 broadcast_multiply_fusion.2
  81.2 9.0 %select_add_fusion.2 = f32[2560,512]{1,0:T(8,128)} fusion(f32[2560,512]{1,0:T(8,128)} %get-tuple-element.236, f32[2560,256]{1,0:T(8,128)S(1)} %bitcast.55, pred[]{:T(512)S(6)} %compare.9, s32[256]{0:T(256)S(1)} %bitcast.69), kind=kOutput, calls=%fused_computation.4.clone.1 | convolution fusion | flops 4032036864 | bytes 13108225 | tf_op jit(solution)/shard_map/while/body/eval_jaxpr/dot_general | solution.py:82
  90.2 0.6 dynamic_slice.18
  91.6 0.2 exponential_select_fusion.2
  91.8 0.3 broadcast_multiply_fusion.2
  92.1 9.0 %select_add_fusion.2 = f32[2560,512]{1,0:T(8,128)} fusion(f32[2560,512]{1,0:T(8,128)} %get-tuple-element.236, f32[2560,256]{1,0:T(8,128)S(1)} %bitcast.55, pred[]{:T(512)S(6)} %compare.9, s32[256]{0:T(256)S(1)} %bitcast.69), kind=kOutput, calls=%fused_computation.4.clone.1 | convolution fusion | flops 4032036864 | bytes 13108225 | tf_op jit(solution)/shard_map/while/body/eval_jaxpr/dot_general | solution.py:82
  101.1 0.6 dynamic_slice.18
  102.7 0.3 broadcast_multiply_fusion.2
  103.0 9.0 %select_add_fusion.2 = f32[2560,512]{1,0:T(8,128)} fusion(f32[2560,512]{1,0:T(8,128)} %get-tuple-element.236, f32[2560,256]{1,0:T(8,128)S(1)} %bitcast.55, pred[]{:T(512)S(6)} %compare.9, s32[256]{0:T(256)S(1)} %bitcast.69), kind=kOutput, calls=%fused_computation.4.clone.1 | convolution fusion | flops 4032036864 | bytes 13108225 | tf_op jit(solution)/shard_map/while/body/eval_jaxpr/dot_general | solution.py:82
  112.0 0.6 dynamic_slice.18
  113.6 0.3 broadcast_multiply_fusion.2
  113.9 9.0 %select_add_fusion.2 = f32[2560,512]{1,0:T(8,128)} fusion(f32[2560,512]{1,0:T(8,128)} %get-tuple-element.236, f32[2560,256]{1,0:T(8,128)S(1)} %bitcast.55, pred[]{:T(512)S(6)} %compare.9, s32[256]{0:T(256)S(1)} %bitcast.69), kind=kOutput, calls=%fused_computation.4.clone.1 | convolution fusion | flops 4032036864 | bytes 13108225 | tf_op jit(solution)/shard_map/while/body/eval_jaxpr/dot_general | solution.py:82
  122.9 0.6 dynamic_slice.18
  124.5 0.3 broadcast_multiply_fusion.2
  124.8 9.0 %select_add_fusion.2 = f32[2560,512]{1,0:T(8,128)} fusion(f32[2560,512]{1,0:T(8,128)} %get-tuple-element.236, f32[2560,256]{1,0:T(8,128)S(1)} %bitcast.55, pred[]{:T(512)S(6)} %compare.9, s32[256]{0:T(256)S(1)} %bitcast.69), kind=kOutput, calls=%fused_computation.4.clone.1 | convolution fusion | flops 4032036864 | bytes 13108225 | tf_op jit(solution)/shard_map/while/body/eval_jaxpr/dot_general | solution.py:82
  133.8 0.6 dynamic_slice.18
  135.4 0.3 broadcast_multiply_fusion.2
  135.7 9.0 %select_add_fusion.2 = f32[2560,512]{1,0:T(8,128)} fusion(f32[2560,512]{1,0:T(8,128)} %get-tuple-element.236, f32[2560,256]{1,0:T(8,128)S(1)} %bitcast.55, pred[]{:T(512)S(6)} %compare.9, s32[256]{0:T(256)S(1)} %bitcast.69), kind=kOutput, calls=%fused_computation.4.clone.1 | convolution fusion | flops 4032036864 | bytes 13108225 | tf_op jit(solution)/shard_map/while/body/eval_jaxpr/dot_general | solution.py:82
  144.7 0.6 dynamic_slice.18
  146.3 0.3 broadcast_multiply_fusion.2
  146.6 9.0 %select_add_fusion.2 = f32[2560,512]{1,0:T(8,128)} fusion(f32[2560,512]{1,0:T(8,128)} %get-tuple-element.236, f32[2560,256]{1,0:T(8,128)S(1)} %bitcast.55, pred[]{:T(512)S(6)} %compare.9, s32[256]{0:T(256)S(1)} %bitcast.69), kind=kOutput, calls=%fused_computation.4.clone.1 | convolution fusion | flops 4032036864 | bytes 13108225 | tf_op jit(solution)/shard_map/while/body/eval_jaxpr/dot_general | solution.py:82
  155.6 3.2 %fusion.57 = (f32[512,512]{1,0:T(8,128)S(1)}, f32[512,512]{1,0:T(8,128)S(1)}, f32[512,512]{1,0:T(8,128)S(1)}, f32[512,512]{1,0:T(8,128)S(1)}, f32[512,512]{1,0:T(8,128)S(1)}) fusion(f32[2560,512]{1,0:T(8,128)} %get-tuple-element.118), kind=kLoop, calls=%fused_computation.99 | loop fusion | bytes 10485760 | tf_op jit(solution)/shard_map/slice | solution.py:167
  158.8 6.2 %collective-permute-start.1 = (f32[4,128,512]{2,1,0:T(8,128)S(1)}, f32[4,128,512]{2,1,0:T(8,128)S(1)}, u32[]{:S(2)}, u32[]{:S(2)}) collective-permute-start(f32[4,128,512]{2,1,0:T(8,128)S(1)} %bitcast.62), channel_id=1, source_target_pairs={{4,0},{8,4},{12,8},{16,12},{20,16},{24,20},{28,24},{32,28},{36,32}... | collective-permute-start | bytes 3145736 | tf_op jit(solution)/shard_map/ppermute | solution.py:43
  164.9 3.1 %collective-permute-start = (f32[4,128,512]{2,1,0:T(8,128)S(1)}, f32[4,128,512]{2,1,0:T(8,128)S(1)}, u32[]{:S(2)}, u32[]{:S(2)}) collective-permute-start(f32[4,128,512]{2,1,0:T(8,128)S(1)} %bitcast.61), channel_id=1, source_target_pairs={{8,0},{12,4},{16,8},{20,12},{24,16},{28,20},{32,24},{36,28},{40,32... | collective-permute-start | bytes 3145736 | tf_op jit(solution)/shard_map/ppermute | solution.py:43
  168.0 2.2 collective-permute-start.3
  170.2 2.7 %collective-permute-start.2 = (f32[4,128,512]{2,1,0:T(8,128)S(1)}, f32[4,128,512]{2,1,0:T(8,128)S(1)}, u32[]{:S(2)}, u32[]{:S(2)}) collective-permute-start(f32[4,128,512]{2,1,0:T(8,128)S(1)} %bitcast.59), channel_id=1, source_target_pairs={{508,0},{0,4},{4,8},{8,12},{12,16},{16,20},{20,24},{24,28},{28,32}... | collective-permute-start | bytes 3145736 | tf_op jit(solution)/shard_map/ppermute | solution.py:43
  172.9 13.3 %collective-permute-done.1 = f32[4,128,512]{2,1,0:T(8,128)S(1)} collective-permute-done((f32[4,128,512]{2,1,0:T(8,128)S(1)}, f32[4,128,512]{2,1,0:T(8,128)S(1)}, u32[]{:S(2)}, u32[]{:S(2)}) %collective-permute-start.1) | collective-permute-done | bytes 1048608 | tf_op jit(solution)/shard_map/ppermute | solution.py:43
  186.2 5.8 %collective-permute-done = f32[4,128,512]{2,1,0:T(8,128)S(1)} collective-permute-done((f32[4,128,512]{2,1,0:T(8,128)S(1)}, f32[4,128,512]{2,1,0:T(8,128)S(1)}, u32[]{:S(2)}, u32[]{:S(2)}) %collective-permute-start) | collective-permute-done | bytes 1048608 | tf_op jit(solution)/shard_map/ppermute | solution.py:43
  192.0 5.7 %collective-permute-done.3 = f32[4,128,512]{2,1,0:T(8,128)S(1)} collective-permute-done((f32[4,128,512]{2,1,0:T(8,128)S(1)}, f32[4,128,512]{2,1,0:T(8,128)S(1)}, u32[]{:S(2)}, u32[]{:S(2)}) %collective-permute-start.3) | collective-permute-done | bytes 1048608 | tf_op jit(solution)/shard_map/ppermute | solution.py:43
  197.7 6.7 %collective-permute-done.2 = f32[4,128,512]{2,1,0:T(8,128)S(1)} collective-permute-done((f32[4,128,512]{2,1,0:T(8,128)S(1)}, f32[4,128,512]{2,1,0:T(8,128)S(1)}, u32[]{:S(2)}, u32[]{:S(2)}) %collective-permute-start.2) | collective-permute-done | bytes 1048608 | tf_op jit(solution)/shard_map/ppermute | solution.py:43
  204.4 1.4 fusion.56
  205.8 12.2 %pmax.28 = f32[]{:T(128)} all-reduce(f32[]{:T(128)} %get-tuple-element.162), channel_id=1, replica_groups=mesh['slab_0'=8,'slab_1'=8,'slab_2'=2,'walk'=4] {'slab_0'}, use_global_device_ids=true, to_apply=%region_6.7 | all-reduce | flops 1 | bytes 8 | tf_op jit(solution)/shard_map/pmax | solution.py:48
  218.0 15.4 %pmax.29 = f32[]{:T(128)} all-reduce(f32[]{:T(128)} %pmax.28), channel_id=1, replica_groups=mesh['slab_0'=8,'slab_1'=8,'slab_2'=2,'walk'=4] {'slab_1'}, use_global_device_ids=true, to_apply=%region_7.8 | all-reduce | flops 1 | bytes 8 | tf_op jit(solution)/shard_map/pmax | solution.py:48
  233.3 10.4 %pmax.30 = f32[]{:T(128)} all-reduce(f32[]{:T(128)} %pmax.29), channel_id=1, replica_groups=mesh['slab_0'=8,'slab_1'=8,'slab_2'=2,'walk'=4] {'slab_2'}, use_global_device_ids=true, to_apply=%region_8.9 | all-reduce | flops 1 | bytes 8 | tf_op jit(solution)/shard_map/pmax | solution.py:48
  243.7 7.6 %pmax.31 = f32[]{:T(128)} all-reduce(f32[]{:T(128)} %pmax.30), channel_id=1, replica_groups=mesh['slab_0'=8,'slab_1'=8,'slab_2'=2,'walk'=4] {'walk'}, use_global_device_ids=true, to_apply=%region_9.10 | all-reduce | flops 1 | bytes 8 | tf_op jit(solution)/shard_map/pmax | solution.py:48
  251.3 1.8 subtract_multiply_fusion
  (70 shorter events, 3.3 us)
Async XLA Ops:
  41.5 8.3 %all-to-all-start.1 = ((f32[4,4,512]{2,1,0:T(4,128)}), f32[4,4,512]{2,1,0:T(4,128)S(1)}, u32[]{:S(2)}, u32[]{:S(2)}) async-start(f32[4,4,512]{2,1,0:T(4,128)} %broadcast_in_dim.69), calls=%async_computation.1 | async-start | bytes 65536 | tf_op jit(solution)/shard_map/all_to_all | solution.py:27
  62.4 7.5 %all-to-all-start.2 = ((f32[4,1,2048]{2,1,0:T(1,128)}), f32[4,1,2048]{2,1,0:T(1,128)S(1)}, u32[]{:S(2)}, u32[]{:S(2)}) async-start(f32[4,1,2048]{2,1,0:T(1,128)} %broadcast_in_dim.71), calls=%async_computation.2 | async-start | bytes 65536 | tf_op jit(solution)/shard_map/all_to_all | solution.py:27
  155.6 48.8 %copy-start.1 = (f32[4,128,512]{2,1,0:T(8,128)S(1)}, f32[4,128,512]{2,1,0:T(8,128)}, u32[]{:S(2)}) copy-start(f32[4,128,512]{2,1,0:T(8,128)} %param.10) | copy-start | bytes 3145732
  158.8 27.5 %collective-permute-start.1 = (f32[4,128,512]{2,1,0:T(8,128)S(1)}, f32[4,128,512]{2,1,0:T(8,128)S(1)}, u32[]{:S(2)}, u32[]{:S(2)}) collective-permute-start(f32[4,128,512]{2,1,0:T(8,128)S(1)} %bitcast.62), channel_id=1, source_target_pairs={{4,0},{8,4},{12,8},{16,12},{20,16},{24,20},{28,24},{32,28},{36,32}... | collective-permute-start | bytes 3145736 | tf_op jit(solution)/shard_map/ppermute | solution.py:43
  164.9 27.1 %collective-permute-start = (f32[4,128,512]{2,1,0:T(8,128)S(1)}, f32[4,128,512]{2,1,0:T(8,128)S(1)}, u32[]{:S(2)}, u32[]{:S(2)}) collective-permute-start(f32[4,128,512]{2,1,0:T(8,128)S(1)} %bitcast.61), channel_id=1, source_target_pairs={{8,0},{12,4},{16,8},{20,12},{24,16},{28,20},{32,24},{36,28},{40,32... | collective-permute-start | bytes 3145736 | tf_op jit(solution)/shard_map/ppermute | solution.py:43
  168.0 29.6 %collective-permute-start.3 = (f32[4,128,512]{2,1,0:T(8,128)S(1)}, f32[4,128,512]{2,1,0:T(8,128)S(1)}, u32[]{:S(2)}, u32[]{:S(2)}) collective-permute-start(f32[4,128,512]{2,1,0:T(8,128)S(1)} %bitcast.60), channel_id=1, source_target_pairs={{504,0},{508,4},{0,8},{4,12},{8,16},{12,20},{16,24},{20,28},{24,32... | collective-permute-start | bytes 3145736 | tf_op jit(solution)/shard_map/ppermute | solution.py:43
  170.2 34.2 %collective-permute-start.2 = (f32[4,128,512]{2,1,0:T(8,128)S(1)}, f32[4,128,512]{2,1,0:T(8,128)S(1)}, u32[]{:S(2)}, u32[]{:S(2)}) collective-permute-start(f32[4,128,512]{2,1,0:T(8,128)S(1)} %bitcast.59), channel_id=1, source_target_pairs={{508,0},{0,4},{4,8},{8,12},{12,16},{16,20},{20,24},{24,28},{28,32}... | collective-permute-start | bytes 3145736 | tf_op jit(solution)/shard_map/ppermute | solution.py:43
  205.8 47.3 %copy-start = (f32[4,128,512]{2,1,0:T(8,128)}, f32[4,128,512]{2,1,0:T(8,128)S(1)}, u32[]{:S(2)}) copy-start(f32[4,128,512]{2,1,0:T(8,128)S(1)} %get-tuple-element.163) | copy-start | bytes 3145732
where the time goes:
time: 255 us; the launch traced here: 253 us
  blocking collectives  78 us (31%)
  matrix products  70.5 us (28%)
  waiting for transfers between devices  38.5 us (15%)
  local copies, waits for them, and re-layouts  25.5 us (10%)
  starting transfers between devices  21.4 us (8%)
  other arithmetic  12.7 us (5%)
  loops' own time  5.57 us (2%)
    dot_general x8, matrix products, one_block(): jnp.dot(plane_gauss, depth_gauss, precision=lax.Precision.HIGHEST, prefer...  70.3 us
    pmax x4, blocking collectives, by_axis(): array = lax.pmax(array, axis)  45.5 us
    all_to_all x1, blocking collectives, per_device(): lax.all_to_all(outgoing, SLAB, split_axis=1, concat_axis=1, tiled=True)  32.5 us
    ppermute x4, waiting for transfers between devices, from_behind(): return lax.ppermute(block, axis, route)  31.5 us
    ppermute x4, starting transfers between devices, from_behind(): return lax.ppermute(block, axis, route)  14.1 us
    gather x1, local copies, waits for them, and re-layouts, per_device(): picked = bias_grid.reshape(-1)[flat_place]  11.8 us
    all_to_all x2, starting transfers between devices, copy_for_each(): lax.all_to_all(jnp.broadcast_to(array[None], (peers, *array.shape)), axis...  7.28 us
    all_to_all x2, waiting for transfers between devices, copy_for_each(): lax.all_to_all(jnp.broadcast_to(array[None], (peers, *array.shape)), axis...  6.96 us
  transfers between devices with their start and end apart: 6, of which 6 were waited for; matrix products, arithmetic and copies ran while one was open for 1% of the time, Pallas kernels for 0%

commit v1 on v0

v1 whole, which is shorter than its diff:
```python
import functools

import jax
import jax.numpy as jnp
from jax import lax
from jax.experimental import pallas as pl
from jax.experimental.pallas import tpu as pltpu
from jax.sharding import Mesh
from jax.sharding import PartitionSpec as P

SLAB = ("y", "z", "c")
CHIP_ROW = ("c", "walk")
EVERY = SLAB + ("walk",)

BASE_HEIGHT = 1.2
TEMPER = 4.0
SIGMA_SHARE = 0.3125
FREE_SCALE = 10.0 / 9.0

LANES = 128
SLOTS = 4
NEAR = 5
FIELD = 32
UNIT = 32

F32 = jnp.float32
BF16 = jnp.bfloat16
I32 = jnp.int32


def iota(shape, dim, dtype=I32):
    return lax.broadcasted_iota(dtype, shape, dim)


def parts_of(x, count):
    parts = []
    for i in range(count):
        part = x.astype(BF16)
        parts.append(part)
        if i + 1 < count:
            x = x - part.astype(F32)
    return parts


def dot_t(a, b):
    return lax.dot_general(a, b, (((1,), (1,)), ((), ())), preferred_element_type=F32)


def dot(a, b):
    return jnp.dot(a, b, preferred_element_type=F32)


def pack_kernel(rows_dev, count, levels, slab, row, col, depth, level, out):
    walkers, hills = slab.shape
    n_slab = out.shape[1]

    def flat(ref):
        return jnp.concatenate([ref[w : w + 1, :] for w in range(walkers)], axis=1)

    total = walkers * hills
    index = iota((1, total), 1)
    limit = jnp.full((1, total), count[0], I32)
    for w in range(1, walkers):
        limit = jnp.where(index < w * hills, limit, count[w] + w * hills)
    live = index < limit
    target = flat(slab)
    lev = flat(level)
    base = jnp.zeros((1, total), F32)
    for i in range(levels.shape[0]):
        base = jnp.where(lev == i, levels[i], base)
    base = jnp.where(live, BASE_HEIGHT * base, 0.0)
    fields = [
        base,
        (target * rows_dev + flat(row)).astype(F32),
        flat(col).astype(F32),
        flat(depth).astype(F32),
    ]
    match = iota((n_slab, total), 0) == target
    earlier = (iota((total, total), 0) < iota((total, total), 1)).astype(F32).astype(BF16)
    rank = dot(match.astype(F32).astype(BF16), earlier)
    rank = jnp.where(match, rank, -1.0)
    place = iota((LANES, total), 0)
    masks, values = [], []
    for slot in range(SLOTS):
        masks.append((rank == slot).astype(F32).astype(BF16))
        value = jnp.zeros((LANES, total), F32)
        for f, field in enumerate(fields):
            value = jnp.where(place == f * FIELD + slot, field, value)
        values.append(value)
    mask = jnp.concatenate(masks, axis=1)
    own = jnp.zeros((n_slab, LANES), F32)
    for part in parts_of(jnp.concatenate(values, axis=1), 3):
        own = own + dot_t(mask, part)
    message = jnp.zeros((n_slab, LANES), F32)
    for k in range(NEAR):
        part = pltpu.roll(own, (NEAR // 2 - k) % n_slab, 0)
        message = message + (pltpu.roll(part, k * SLOTS, 1) if k else part)
    for w in range(out.shape[0]):
        out[w] = message


def positions(active, chain, block):
    earlier = (iota((LANES, LANES), 0) < iota((LANES, LANES), 1)).astype(F32).astype(BF16)
    ones = jnp.ones((LANES, LANES), F32).astype(BF16)
    found, most = [], None
    for j in range(block):
        a = active[:, j * LANES : (j + 1) * LANES]
        ab = a.astype(BF16)
        total = dot(ab, ones)
        ahead = dot(chain, total.astype(BF16))
        found.append(jnp.where(a > 0.0, dot(ab, earlier) + ahead, -1.0))
        count = ahead + total
        most = count if most is None else jnp.maximum(most, count)
    return found, jnp.max(most).astype(I32)


def chain_of(rows):
    i, j = iota((rows, rows), 0), iota((rows, rows), 1)
    same = lax.shift_right_logical(i, 2) == lax.shift_right_logical(j, 2)
    return (same & (j < i)).astype(F32).astype(BF16)


def height_kernel(rows_dev, cols_dev, grid_cols, recv, bias, out, table, hi, mid, lo, found):
    senders = recv.shape[0]
    blocks = senders // LANES
    cells, depth_bins = bias.shape
    walk = lax.axis_index("walk")
    for j in range(blocks):
        table[:, j * LANES : (j + 1) * LANES] = recv[j * LANES : (j + 1) * LANES, :].T
    first = (NEAR // 2) * SLOTS
    base = table[first : first + 8, :]
    row = table[FIELD + first : FIELD + first + 8, :].astype(I32)
    col = table[2 * FIELD + first : 2 * FIELD + first + 8, :].astype(I32)
    depth = table[3 * FIELD + first : 3 * FIELD + first + 8, :]
    col = col - walk * cols_dev
    held = (iota(base.shape, 0) < SLOTS) & (base != 0.0) & (col >= 0) & (col < cols_dev)
    cell = ((row & (rows_dev - 1)) * cols_dev + col).astype(F32)
    place, most = positions(held.astype(F32), chain_of(8), blocks)
    bias_parts = parts_of(bias[...], 3)
    hi[...], mid[...], lo[...] = bias_parts
    found[...] = jnp.zeros_like(found)

    def one_pass(t, carry):
        number = (iota((UNIT, LANES), 0) + t * UNIT).astype(F32)
        cells_at, depths_at, hits = [], [], []
        for j in range(blocks):
            at = slice(j * LANES, (j + 1) * LANES)
            c = jnp.zeros((UNIT, LANES), F32)
            d = jnp.zeros((UNIT, LANES), F32)
            for slot in range(SLOTS):
                hit = place[j][slot : slot + 1, :] == number
                hits.append(hit)
                c = jnp.where(hit, cell[slot : slot + 1, at], c)
                d = jnp.where(hit, depth[slot : slot + 1, at], d)
            cells_at.append(jnp.sum(c, axis=1, keepdims=True))
            depths_at.append(jnp.sum(d, axis=1, keepdims=True))
        cells_at = jnp.concatenate(cells_at, axis=0).astype(I32)
        depths_at = jnp.concatenate(depths_at, axis=0).astype(I32)
        count = blocks * UNIT
        pick = (iota((count, cells), 1) == cells_at).astype(F32).astype(BF16)
        lines = dot(pick, hi[...]) + dot(pick, mid[...]) + dot(pick, lo[...])
        value = jnp.sum(
            jnp.where(iota((count, depth_bins), 1) == depths_at, lines, 0.0),
            axis=1,
            keepdims=True,
        )
        for j in range(blocks):
            v = value[j * UNIT : (j + 1) * UNIT, :]
            for slot in range(SLOTS):
                back = jnp.sum(
                    jnp.where(hits[j * SLOTS + slot], v, 0.0), axis=0, keepdims=True
                )
                found[slot : slot + 1, j * LANES : (j + 1) * LANES] += back
        return carry

    lax.fori_loop(0, lax.div(most + (UNIT - 1), UNIT), one_pass, 0)
    height = jnp.where(held, base * jnp.exp(-found[...] / TEMPER), 0.0)
    for i in range(out.shape[0]):
        out[i] = height[:SLOTS, :]


def profile(offset, radius, extent):
    spread = SIGMA_SHARE * radius
    shifted = (offset + radius) & (extent - 1)
    t = (shifted - radius).astype(F32)
    return jnp.where(shifted < 2 * radius, jnp.exp(-(t * t) / (2.0 * spread * spread)), 0.0)


def deposit_kernel(
    rows_dev, cols_dev, grid_rows, grid_cols, radius,
    table, below, own, above, bias, out, peak, lists, heights, rows_of, row_hi, row_lo, col_hi, col_lo,
):
    senders = table.shape[1]
    blocks = senders // LANES
    cells, depth_bins = bias.shape
    slab = lax.axis_index(SLAB)
    walk = lax.axis_index("walk")
    start = lax.axis_index("c")
    chip = own.shape[0]
    for i in range(chip):
        lists[i] = below[i]
        lists[chip + i] = own[i]
        lists[2 * chip + i] = above[i]
    used = 8 * ((NEAR * SLOTS + 7) // 8)
    heights[...] = jnp.zeros_like(heights)
    for k in range(NEAR):
        heights[k * SLOTS : (k + 1) * SLOTS, :] = lists[start + k]
    base = table[0:used, :]
    row = table[FIELD : FIELD + used, :]
    col = table[2 * FIELD : 2 * FIELD + used, :]
    depth = table[3 * FIELD : 3 * FIELD + used, :]
    reached = ((col.astype(I32) - walk * cols_dev + (radius - 1)) & (grid_cols - 1)) < (
        cols_dev + 2 * radius - 1
    )
    active = (iota(base.shape, 0) < NEAR * SLOTS) & (base != 0.0) & reached
    place, most = positions(active.astype(F32), chain_of(used), blocks)
    count = NEAR * blocks * UNIT
    chunks = count // LANES
    out[...] = bias[...]

    def one_pass(t, carry):
        number = (iota((UNIT, LANES), 0) + t * UNIT).astype(F32)
        lane = iota((UNIT, LANES), 1)
        for k in range(NEAR):
            for j in range(blocks):
                at = slice(j * LANES, (j + 1) * LANES)
                sums = [jnp.zeros((UNIT, LANES), F32) for _ in range(4)]
                for slot in range(SLOTS):
                    i = k * SLOTS + slot
                    hit = place[j][i : i + 1, :] == number
                    for f, field in enumerate((row, col, depth, heights)):
                        sums[f] = jnp.where(hit, field[i : i + 1, at], sums[f])
                cols = [jnp.sum(s, axis=1, keepdims=True) for s in sums]
                packed = jnp.where(
                    lane == 0,
                    cols[0],
                    jnp.where(lane == 1, cols[1], jnp.where(lane == 2, cols[2], cols[3])),
                )
                u = (k * blocks + j) * UNIT
                rows_of[u : u + UNIT, :] = packed
        for h in range(chunks):
            at = slice(h * LANES, (h + 1) * LANES)
            block = rows_of[at, :]
            turned = block.T
            row_at = turned[0:1, :].astype(I32)
            col_at = turned[1:2, :].astype(I32)
            height_at = turned[3:4, :]
            depth_at = block[:, 2:3].astype(I32)
            col_part = profile(
                iota((cols_dev, LANES), 0) + walk * cols_dev - col_at, radius, grid_cols
            )
            for r in range(rows_dev):
                row_part = profile(slab * rows_dev + r - row_at, radius, grid_rows) * height_at
                first, second = parts_of(col_part * row_part, 2)
                row_hi[r * cols_dev : (r + 1) * cols_dev, at] = first
                row_lo[r * cols_dev : (r + 1) * cols_dev, at] = second
            first, second = parts_of(
                profile(iota((LANES, depth_bins), 1) - depth_at, radius, depth_bins), 2
            )
            col_hi[at, :] = first
            col_lo[at, :] = second
        added = dot(row_hi[...], col_lo[...]) + dot(row_lo[...], col_hi[...])
        out[...] += added + dot(row_hi[...], col_hi[...])
        return carry

    lax.fori_loop(0, lax.div(most + (UNIT - 1), UNIT), one_pass, 0)
    peak[...] = jnp.full(peak.shape, jnp.max(out[...]), F32)


def spread_max_kernel(recv, out):
    out[...] = jnp.full(out.shape, jnp.max(recv[...]), F32)


def free_kernel(recv, bias, out):
    out[...] = FREE_SCALE * (jnp.max(recv[...]) - bias[...])


def call(body, name, out_shape, *operands, smem=0, scratch=()):
    in_specs = [
        pl.BlockSpec(memory_space=pltpu.SMEM if i < smem else pltpu.VMEM)
        for i in range(len(operands))
    ]
    out_specs = jax.tree.map(lambda s: pl.BlockSpec(memory_space=pltpu.VMEM), out_shape)
    return pl.pallas_call(
        body,
        name=name,
        out_shape=out_shape,
        in_specs=in_specs,
        out_specs=out_specs,
        scratch_shapes=list(scratch),
    )(*operands)


def shape_of(*dims):
    return jax.ShapeDtypeStruct(dims, F32)


def swap(array, axes):
    return lax.all_to_all(array, axes, 0, 0, tiled=True)


def per_device(
    bias_grid, hill_slab, hill_row, hill_col, hill_depth, hill_level, hill_count, height_levels
):
    rows_dev, cols_dev, depth_bins = bias_grid.shape
    n_slab = lax.axis_size(SLAB)
    n_walk = lax.axis_size("walk")
    radius = 2 * rows_dev
    grid_rows = rows_dev * n_slab
    grid_cols = cols_dev * n_walk
    senders = n_slab * n_walk
    cells = rows_dev * cols_dev
    chip = lax.axis_size("c")
    bias = bias_grid.reshape(cells, depth_bins)

    message = call(
        functools.partial(pack_kernel, rows_dev),
        "pack",
        shape_of(n_walk, n_slab, LANES),
        hill_count,
        height_levels,
        hill_slab[:, :, 0],
        hill_row,
        hill_col,
        hill_depth,
        hill_level,
        smem=2,
    )
    recv = swap(message.reshape(senders, 1, LANES), ("walk",) + SLAB).reshape(senders, LANES)

    own, table = call(
        functools.partial(height_kernel, rows_dev, cols_dev, grid_cols),
        "heights",
        (shape_of(chip * n_walk, SLOTS, senders), shape_of(LANES, senders)),
        recv,
        bias,
        scratch=[pltpu.VMEM((cells, depth_bins), BF16)] * 3 + [pltpu.VMEM((8, senders), F32)],
    )
    own = swap(own, CHIP_ROW).reshape(chip, n_walk, SLOTS, senders).sum(axis=1)
    ring = range(n_slab)
    below = lax.ppermute(own, SLAB, [(s, (s + chip) % n_slab) for s in ring])
    above = lax.ppermute(own, SLAB, [(s, (s - chip) % n_slab) for s in ring])

    hills = NEAR * (senders // LANES) * UNIT
    used = 8 * ((NEAR * SLOTS + 7) // 8)
    new_bias, peak = call(
        functools.partial(deposit_kernel, rows_dev, cols_dev, grid_rows, grid_cols, radius),
        "deposit",
        (shape_of(cells, depth_bins), shape_of(lax.axis_size(("z", "c")), LANES)),
        table,
        below,
        own,
        above,
        bias,
        scratch=[
            pltpu.VMEM((3 * chip, SLOTS, senders), F32),
            pltpu.VMEM((used, senders), F32),
            pltpu.VMEM((hills, LANES), F32),
            pltpu.VMEM((cells, hills), BF16),
            pltpu.VMEM((cells, hills), BF16),
            pltpu.VMEM((hills, depth_bins), BF16),
            pltpu.VMEM((hills, depth_bins), BF16),
        ],
    )
    near = ("z", "c")
    far = ("y", "walk")
    n_near, n_far = lax.axis_size(near), lax.axis_size(far)
    peaks = swap(peak.reshape(n_near, 1, LANES), near).reshape(n_near, LANES)
    peaks = call(spread_max_kernel, "spread", shape_of(n_far, LANES), peaks)
    peaks = swap(peaks.reshape(n_far, 1, LANES), far).reshape(n_far, LANES)
    free = call(free_kernel, "free", shape_of(cells, depth_bins), peaks, new_bias)
    return new_bias.reshape(bias_grid.shape), free.reshape(bias_grid.shape)


def solution(mesh):
    split = Mesh(mesh.devices.reshape(8, 8, 2, mesh.shape["walk"]), EVERY)
    in_specs = (
        P(SLAB, "walk", None),
        P(EVERY, None, None),
        P(EVERY, None),
        P(EVERY, None),
        P(EVERY, None),
        P(EVERY, None),
        P(EVERY),
        P(),
    )
    out_specs = (P(SLAB, "walk", None), P(SLAB, "walk", None))
    return jax.shard_map(
        per_device, mesh=split, in_specs=in_specs, out_specs=out_specs, check_vma=False
    )
```

time: 255 us -> 107 us (0.42)
  matrix products: 70.5 us -> 0 us
  waiting for transfers between devices: 38.5 us -> 5.44 us
  local copies, waits for them, and re-layouts: 25.5 us -> 0.6 us
  Pallas kernels: 0 us -> 18 us
  starting transfers between devices: 21.4 us -> 5.83 us
  other arithmetic: 12.7 us -> 0.02 us
  loops' own time: 5.57 us -> 0 us
    dot_general x9 -> x0, matrix products: 70.5 us -> none  [the longest x8 70.3 us: one_block(): jnp.dot(plane_gauss, depth_gauss, precision=lax.Precision.HIGHEST, prefer...]
    pmax x4 -> x0, blocking collectives: 45.5 us -> none  [by_axis(): array = lax.pmax(array, axis)]
    all_to_all x1 -> x4, blocking collectives: 32.5 us -> 76.2 us  [swap(): return lax.all_to_all(array, axes, 0, 0, tiled=True)]
    ppermute x4 -> x2, waiting for transfers between devices: 31.5 us -> 5.44 us  [the longest x1 5.44 us: per_device(): below = lax.ppermute(own, SLAB, [(s, (s + chip) % n_slab) for s in ring])]
    pallas_call x0 -> x5, Pallas kernels: none -> 18 us  [call(): pl.pallas_call(body, name=name, out_shape=out_shape, in_specs=in_specs, o...]
    gather x1 -> x0, local copies, waits for them, and re-layouts: 11.8 us -> none  [per_device(): picked = bias_grid.reshape(-1)[flat_place]]
    ppermute x4 -> x2, starting transfers between devices: 14.1 us -> 5.83 us  [the longest x1 3.49 us: per_device(): above = lax.ppermute(own, SLAB, [(s, (s - chip) % n_slab) for s in ring])]
    all_to_all x2 -> x0, starting transfers between devices: 7.28 us -> none  [copy_for_each(): lax.all_to_all(jnp.broadcast_to(array[None], (peers, *array.shape)), axis...]
  transfers between devices with their start and end apart: 6 -> 2, of which waited for: 6 -> 1; matrix products, arithmetic and copies ran while one was open for 1% -> 0% of each run, Pallas kernels for 0% -> 0%
where the time goes in v1:
time: 107 us
  blocking collectives  76.2 us (71%)
  Pallas kernels  18 us (17%)
  starting transfers between devices  5.83 us (5%)
  waiting for transfers between devices  5.44 us (5%)
    all_to_all x4, blocking collectives, swap(): return lax.all_to_all(array, axes, 0, 0, tiled=True)  76.2 us
    pallas_call x5, Pallas kernels, call(): pl.pallas_call(body, name=name, out_shape=out_shape, in_specs=in_specs, o...  18 us
    ppermute x1, waiting for transfers between devices, per_device(): below = lax.ppermute(own, SLAB, [(s, (s + chip) % n_slab) for s in ring])  5.44 us
    ppermute x1, starting transfers between devices, per_device(): above = lax.ppermute(own, SLAB, [(s, (s - chip) % n_slab) for s in ring])  3.49 us
    ppermute x1, starting transfers between devices, per_device(): below = lax.ppermute(own, SLAB, [(s, (s + chip) % n_slab) for s in ring])  2.34 us
  transfers between devices with their start and end apart: 2, of which 1 were waited for; matrix products, arithmetic and copies ran while one was open for 0% of the time, Pallas kernels for 0%

profile of v1, /device:TPU:1, one launch (start us, length us, event | category | flops | bytes accessed | tf_op | source)
XLA Modules:
  0.0 106.8 jit_solution(17170084198820336347)
XLA Ops:
  0.6 2.1 %pack.1 = f32[4,128,128]{2,1,0:T(8,128)} custom-call(s32[2]{0:T(128)} %count.1, f32[8]{0:T(128)} %levels.1, s32[2,64]{1,0:T(2,128)} %bitcast.28, s32[2,64]{1,0:T(2,128)} %row.1, s32[2,64]{1,0:T(2,128)} %col.1, s32[2,64]{1,0:T(2,128)} %depth.1, s32[2,64]{1,0:T(2,128)} %level.1), custom_call_target="tpu_custom_call" | custom-call | tf_op jit(solution)/shard_map/pack/pallas_call | solution.py:284
  2.7 39.2 %all_to_all.20 = f32[512,1,128]{2,1,0:T(1,128)} all-to-all(f32[512,1,128]{2,1,0:T(1,128)} %bitcast.23), channel_id=1, replica_groups=mesh['y'=8,'z'=8,'c'=2,'walk'=4] {'walk','y','z','c'}, dimensions={0} | all-to-all | bytes 524288 | tf_op jit(solution)/shard_map/all_to_all | solution.py:299
  41.9 3.8 %heights.1 = (f32[8,4,512]{2,1,0:T(4,128)}, f32[128,512]{1,0:T(8,128)}) custom-call(f32[512,128]{1,0:T(8,128)} %bitcast.20, f32[512,512]{1,0:T(8,128)} %bitcast.18), custom_call_target="tpu_custom_call" | custom-call | tf_op jit(solution)/shard_map/heights/pallas_call | solution.py:284
  45.7 8.8 %all_to_all.21 = f32[8,4,512]{2,1,0:T(4,128)S(1)} all-to-all(f32[8,4,512]{2,1,0:T(4,128)} %get-tuple-element.7), channel_id=1, replica_groups=mesh['y'=8,'z'=8,'c'=2,'walk'=4] {'c','walk'}, dimensions={0} | all-to-all | bytes 131072 | tf_op jit(solution)/shard_map/all_to_all | solution.py:299
  54.5 0.0 copy-start
  54.6 3.5 %collective-permute-start.1 = (f32[2,4,512]{2,1,0:T(4,128)S(1)}, f32[2,4,512]{2,1,0:T(4,128)S(1)}, u32[]{:S(2)}, u32[]{:S(2)}) collective-permute-start(f32[2,4,512]{2,1,0:T(4,128)S(1)} %bitcast_reduce_fusion.own), channel_id=1, source_target_pairs={{0,504},{4,508},{8,0},{12,4},{16,8},{20,12},{24,16},{28,20},{32,24... | collective-permute-start | bytes 49160 | tf_op jit(solution)/shard_map/ppermute | solution.py:342
  58.1 2.3 %collective-permute-start = (f32[2,4,512]{2,1,0:T(4,128)S(1)}, f32[2,4,512]{2,1,0:T(4,128)S(1)}, u32[]{:S(2)}, u32[]{:S(2)}) collective-permute-start(f32[2,4,512]{2,1,0:T(4,128)S(1)} %bitcast_reduce_fusion.own), channel_id=1, source_target_pairs={{0,8},{4,12},{8,16},{12,20},{16,24},{20,28},{24,32},{28,36},{32,40... | collective-permute-start | bytes 49160 | tf_op jit(solution)/shard_map/ppermute | solution.py:341
  60.4 0.0 collective-permute-done.1.above
  60.4 0.0 copy-start.1
  60.4 5.4 %collective-permute-done.below = f32[2,4,512]{2,1,0:T(4,128)S(1)} collective-permute-done((f32[2,4,512]{2,1,0:T(4,128)S(1)}, f32[2,4,512]{2,1,0:T(4,128)S(1)}, u32[]{:S(2)}, u32[]{:S(2)}) %collective-permute-start) | collective-permute-done | bytes 16416 | tf_op jit(solution)/shard_map/ppermute | solution.py:341
  65.9 0.0 copy-start.2
  65.9 0.0 copy-done
  65.9 0.0 copy-done.1
  65.9 0.6 copy-done.2
  66.5 8.4 %deposit.1 = (f32[512,512]{1,0:T(8,128)}, f32[16,128]{1,0:T(8,128)}) custom-call(f32[128,512]{1,0:T(8,128)} %get-tuple-element.6.table, f32[2,4,512]{2,1,0:T(4,128)} %copy-done.2, f32[2,4,512]{2,1,0:T(4,128)} %copy-done, f32[2,4,512]{2,1,0:T(4,128)} %copy-done.1, f32[512,512]{1,0:T(8,128)} %bitcast.19), custom_call_target="tpu_custom_call" | custom-call | tf_op jit(solution)/shard_map/deposit/pallas_call | solution.py:284
  74.8 14.3 %all_to_all.22 = f32[16,1,128]{2,1,0:T(1,128)} all-to-all(f32[16,1,128]{2,1,0:T(1,128)} %bitcast.27), channel_id=1, replica_groups=mesh['y'=8,'z'=8,'c'=2,'walk'=4] {'z','c'}, dimensions={0} | all-to-all | bytes 16384 | tf_op jit(solution)/shard_map/all_to_all | solution.py:299
  89.1 1.4 %spread.1 = f32[32,128]{1,0:T(8,128)} custom-call(f32[16,128]{1,0:T(8,128)} %bitcast.26), custom_call_target="tpu_custom_call" | custom-call | tf_op jit(solution)/shard_map/spread/pallas_call | solution.py:284
  90.6 13.8 %all_to_all.23 = f32[32,1,128]{2,1,0:T(1,128)} all-to-all(f32[32,1,128]{2,1,0:T(1,128)} %bitcast.25), channel_id=1, replica_groups=mesh['y'=8,'z'=8,'c'=2,'walk'=4] {'y','walk'}, dimensions={0} | all-to-all | bytes 32768 | tf_op jit(solution)/shard_map/all_to_all | solution.py:299
  104.4 2.4 %free.1 = f32[512,512]{1,0:T(8,128)} custom-call(f32[32,128]{1,0:T(8,128)} %bitcast.24, f32[512,512]{1,0:T(8,128)} %get-tuple-element.8.bias), custom_call_target="tpu_custom_call" | custom-call | tf_op jit(solution)/shard_map/free/pallas_call | solution.py:284
  (1 shorter events, 0.0 us)
Async XLA Ops:
  54.5 11.3 %copy-start = (f32[2,4,512]{2,1,0:T(4,128)}, f32[2,4,512]{2,1,0:T(4,128)S(1)}, u32[]{:S(2)}) copy-start(f32[2,4,512]{2,1,0:T(4,128)S(1)} %bitcast_reduce_fusion.own) | copy-start | bytes 49156
  54.6 5.8 %collective-permute-start.1 = (f32[2,4,512]{2,1,0:T(4,128)S(1)}, f32[2,4,512]{2,1,0:T(4,128)S(1)}, u32[]{:S(2)}, u32[]{:S(2)}) collective-permute-start(f32[2,4,512]{2,1,0:T(4,128)S(1)} %bitcast_reduce_fusion.own), channel_id=1, source_target_pairs={{0,504},{4,508},{8,0},{12,4},{16,8},{20,12},{24,16},{28,20},{32,24... | collective-permute-start | bytes 49160 | tf_op jit(solution)/shard_map/ppermute | solution.py:342
  58.1 7.8 %collective-permute-start = (f32[2,4,512]{2,1,0:T(4,128)S(1)}, f32[2,4,512]{2,1,0:T(4,128)S(1)}, u32[]{:S(2)}, u32[]{:S(2)}) collective-permute-start(f32[2,4,512]{2,1,0:T(4,128)S(1)} %bitcast_reduce_fusion.own), channel_id=1, source_target_pairs={{0,8},{4,12},{8,16},{12,20},{16,24},{20,28},{24,32},{28,36},{32,40... | collective-permute-start | bytes 49160 | tf_op jit(solution)/shard_map/ppermute | solution.py:341
  60.4 5.5 %copy-start.1 = (f32[2,4,512]{2,1,0:T(4,128)}, f32[2,4,512]{2,1,0:T(4,128)S(1)}, u32[]{:S(2)}) copy-start(f32[2,4,512]{2,1,0:T(4,128)S(1)} %collective-permute-done.1.above) | copy-start | bytes 49156
  65.9 0.6 copy-start.2

commit v2 on v1

v2 whole, which is shorter than its diff:
```python
import functools

import jax
import jax.numpy as jnp
from jax import lax
from jax.experimental import pallas as pl
from jax.experimental.pallas import tpu as pltpu
from jax.sharding import Mesh
from jax.sharding import PartitionSpec as P

SLAB = ("y", "z", "c")
CHIP_ROW = ("c", "walk")
EVERY = SLAB + ("walk",)

BASE_HEIGHT = 1.2
TEMPER = 4.0
SIGMA_SHARE = 0.3125
FREE_SCALE = 10.0 / 9.0

LANES = 128
SLOTS = 4
CHIP = 2
NEAR = 6
FIELD = 32
UNIT = 32
HELD = 64
CHUNK = 256

F32 = jnp.float32
BF16 = jnp.bfloat16
I32 = jnp.int32


def iota(shape, dim, dtype=I32):
    return lax.broadcasted_iota(dtype, shape, dim)


def parts_of(x, count):
    parts = []
    for i in range(count):
        part = x.astype(BF16)
        parts.append(part)
        if i + 1 < count:
            x = x - part.astype(F32)
    return parts


def dot_t(a, b):
    return lax.dot_general(a, b, (((1,), (1,)), ((), ())), preferred_element_type=F32)


def dot(a, b):
    return jnp.dot(a, b, preferred_element_type=F32)


def pack_kernel(rows_dev, *refs):
    arrays, bias, out, bias_out = refs[:7], refs[7], refs[8], refs[9]
    local, sems = refs[10:17], refs[17]
    bias_copy = pltpu.make_async_copy(bias, bias_out, sems.at[len(arrays)])
    copies = [
        pltpu.make_async_copy(a, b, sems.at[i]) for i, (a, b) in enumerate(zip(arrays, local))
    ]
    for c in copies:
        c.start()
    bias_copy.start()
    for c in copies:
        c.wait()
    count, levels, slab, row, col, depth, level = local
    walkers, hills = slab.shape
    chips = out.shape[0]

    def flat(ref):
        return jnp.concatenate([ref[w : w + 1, :] for w in range(walkers)], axis=1)

    total = walkers * hills
    index = iota((1, total), 1)
    limit = jnp.full((1, total), count[0], I32)
    for w in range(1, walkers):
        limit = jnp.where(index < w * hills, limit, count[w] + w * hills)
    target = flat(slab)
    lev = flat(level)
    base = jnp.zeros((1, total), F32)
    for i in range(levels.shape[0]):
        base = jnp.where(lev == i, levels[i], base)
    base = jnp.where(index < limit, BASE_HEIGHT * base, 0.0)
    fields = [
        base,
        (target * rows_dev + flat(row)).astype(F32),
        flat(col).astype(F32),
        flat(depth).astype(F32),
    ]
    line = iota((CHIP * chips, total), 0)
    match = jnp.where(line < chips, CHIP * line, CHIP * (line - chips) + 1) == target
    rank = dot(match.astype(F32).astype(BF16), ahead_of(total))
    rank = jnp.where(match, rank, -1.0)
    place = iota((LANES, total), 0)
    masks, values = [], []
    for slot in range(SLOTS):
        masks.append((rank == slot).astype(F32).astype(BF16))
        value = jnp.zeros((LANES, total), F32)
        for f, field in enumerate(fields):
            value = jnp.where(place == f * FIELD + slot, field, value)
        values.append(value)
    mask = jnp.concatenate(masks, axis=1)
    own = jnp.zeros((CHIP * chips, LANES), F32)
    for part in parts_of(jnp.concatenate(values, axis=1), 3):
        own = own + dot_t(mask, part)
    message = jnp.zeros((chips, LANES), F32)
    for k in range(NEAR):
        part = own[(k % CHIP) * chips : (k % CHIP + 1) * chips, :]
        part = pltpu.roll(part, (1 - k // CHIP) % chips, 0)
        message = message + (pltpu.roll(part, k * SLOTS, 1) if k else part)
    out[...] = message
    bias_copy.wait()


def ahead_of(size):
    return (iota((size, size), 0) < iota((size, size), 1)).astype(F32).astype(BF16)


def numbered(active):
    rows, senders = active.shape
    i, j = iota((rows, rows), 0), iota((rows, rows), 1)
    same = lax.shift_right_logical(i, 2) == lax.shift_right_logical(j, 2)
    chain = (same & (j < i)).astype(F32).astype(BF16)
    earlier = ahead_of(LANES)
    ones = jnp.ones((LANES, LANES), F32).astype(BF16)
    places, counts = [], []
    for b in range(senders // LANES):
        a = active[:, b * LANES : (b + 1) * LANES]
        ab = a.astype(BF16)
        total = dot(ab, ones)
        ahead = dot(chain, total.astype(BF16))
        places.append(jnp.where(a > 0.0, dot(ab, earlier) + ahead, -1.0))
        counts.append(ahead + total)
    return places, counts


def height_kernel(cols_dev, recv, bias, out, table, hi, lo, found):
    senders = recv.shape[0]
    blocks = senders // LANES
    cells, depth_bins = bias.shape
    rows_dev = cells // cols_dev
    walk = lax.axis_index("walk")
    core = lax.axis_index("c")
    for j in range(blocks):
        table[:, j * LANES : (j + 1) * LANES] = recv[j * LANES : (j + 1) * LANES, :].T
    first = CHIP * SLOTS
    rows = CHIP * SLOTS
    base = table[first : first + rows, :]
    row = table[FIELD + first : FIELD + first + rows, :].astype(I32)
    col = table[2 * FIELD + first : 2 * FIELD + first + rows, :].astype(I32)
    depth = table[3 * FIELD + first : 3 * FIELD + first + rows, :]
    col = col - walk * cols_dev
    mine = lax.shift_right_logical(iota(base.shape, 0), 2) == core
    held = mine & (base != 0.0) & (col >= 0) & (col < cols_dev)
    cell = (row & (rows_dev - 1)) * cols_dev + col
    code = (cell * depth_bins).astype(F32) + depth
    place, counts = numbered(held.astype(F32))
    most = jnp.max(functools.reduce(jnp.maximum, counts)).astype(I32)
    hi[...], lo[...] = parts_of(bias[...], 2)
    found[...] = jnp.zeros_like(found)

    def one_pass(t, carry):
        number = (iota((HELD, LANES), 0) + t * HELD).astype(F32)
        codes, hits = [], []
        for j in range(blocks):
            at = slice(j * LANES, (j + 1) * LANES)
            c = jnp.zeros((HELD, LANES), F32)
            for i in range(rows):
                hit = place[j][i : i + 1, :] == number
                hits.append(hit)
                c = jnp.where(hit, code[i : i + 1, at], c)
            codes.append(jnp.sum(c, axis=1, keepdims=True))
        codes = jnp.concatenate(codes, axis=0).astype(I32)
        count = blocks * HELD
        shift = depth_bins.bit_length() - 1
        pick = iota((count, cells), 1) == lax.shift_right_logical(codes, shift)
        pick = pick.astype(F32).astype(BF16)
        lines = dot(pick, hi[...]) + dot(pick, lo[...])
        there = iota((count, depth_bins), 1) == (codes & (depth_bins - 1))
        value = jnp.sum(jnp.where(there, lines, 0.0), axis=1, keepdims=True)
        for j in range(blocks):
            v = value[j * HELD : (j + 1) * HELD, :]
            for i in range(rows):
                back = jnp.sum(jnp.where(hits[j * rows + i], v, 0.0), axis=0, keepdims=True)
                found[i : i + 1, j * LANES : (j + 1) * LANES] += back
        return carry

    lax.fori_loop(0, lax.div(most + (HELD - 1), HELD), one_pass, 0)
    height = jnp.where(held, base * jnp.exp(-found[...] / TEMPER), 0.0)
    for i in range(out.shape[0]):
        out[i] = height


def in_windows(units, offset, count, write):
    for u in range(units):

        def later(t, carry, u=u):
            write(u, t, pl.multiple_of(offset[u] + t * UNIT, 8))
            return carry

        lax.fori_loop(1, lax.div(count[u] + (UNIT - 1), UNIT), later, 0)
    for u in range(units):
        write(u, 0, pl.multiple_of(offset[u], 8))


def gathered(place, field, u, blocks, t):
    number = (iota((UNIT, LANES), 0) + t * UNIT).astype(F32)
    q, j = u // blocks, u % blocks
    at = slice(j * LANES, (j + 1) * LANES)
    found = jnp.zeros((UNIT, LANES), F32)
    for i in range(q * SLOTS, (q + 1) * SLOTS):
        found = jnp.where(place[i : i + 1, at] == number, field[i : i + 1, at], found)
    return jnp.broadcast_to(jnp.sum(found, axis=1, keepdims=True), (UNIT, LANES))


def list_kernel(cols_dev, grid_cols, rows_dev, radius, depth_bins, table, after, codes, place, units, code):
    senders = table.shape[1]
    blocks = senders // LANES
    rows = NEAR * SLOTS
    walk = lax.axis_index("walk")
    core = lax.axis_index("c")
    base = table[0:rows, :]
    row = table[FIELD : FIELD + rows, :].astype(I32)
    col = table[2 * FIELD : 2 * FIELD + rows, :].astype(I32)
    depth = table[3 * FIELD : 3 * FIELD + rows, :].astype(I32)
    line = iota(base.shape, 0)
    col = (col - walk * cols_dev + (radius - 1)) & (grid_cols - 1)
    near = lax.shift_right_logical(line, 2)
    reached = (near >= core) & (near < core + NEAR - 1) & (col < cols_dev + 2 * radius - 1)
    active = reached & (base != 0.0)
    row = near * rows_dev + (row & (rows_dev - 1))
    code[...] = ((row * 256 + col) * depth_bins + depth).astype(F32)
    places, counts = numbered(active.astype(F32))
    for j in range(blocks):
        place[:, j * LANES : (j + 1) * LANES] = places[j]
    total = jnp.int32(0)
    n_units = NEAR * blocks
    for u in range(n_units):
        i = (u // blocks) * SLOTS + SLOTS - 1
        n = jnp.max(counts[u % blocks][i : i + 1, :]).astype(I32)
        units[0, u] = total
        units[1, u] = n
        total = total + ((n + 7) & -8)
    units[0, n_units] = total

    def write(u, t, row):
        codes[pl.ds(row, UNIT), :] = gathered(place, code, u, blocks, t)

    in_windows(n_units, units.at[0], units.at[1], write)


def profile(shifted, radius):
    spread = SIGMA_SHARE * radius
    t = (shifted - radius).astype(F32)
    within = (shifted >= 0) & (shifted < 2 * radius)
    return jnp.where(within, jnp.exp(-(t * t) / (2.0 * spread * spread)), 0.0)


def deposit_kernel(
    rows_dev, cols_dev, radius,
    units, codes, place, below, own, above, bias, out, peak,
    heights, height, row_hi, row_lo, col_hi, col_lo,
):
    blocks = place.shape[1] // LANES
    cells, depth_bins = bias.shape
    core = lax.axis_index("c")
    rows = CHIP * SLOTS
    heights[0:rows, :] = below[...]
    heights[rows : 2 * rows, :] = own[...]
    heights[2 * rows : 3 * rows, :] = above[...]
    n_units = NEAR * blocks

    def write(u, t, row):
        height[pl.ds(row, UNIT), :] = gathered(place, heights, u, blocks, t)

    in_windows(n_units, units.at[0], units.at[1], write)
    total = units[0, n_units]
    out[...] = bias[...]

    def one_chunk(g, carry):
        start = pl.multiple_of(g * CHUNK, CHUNK)
        live = iota((CHUNK, LANES), 0) + start < total
        code = jnp.where(live, codes[pl.ds(start, CHUNK), :], 0.0)
        high = jnp.where(live, height[pl.ds(start, CHUNK), :], 0.0)[:, 0:1]
        depth = code[:, 0:1].astype(I32) & (depth_bins - 1)
        turned = jnp.concatenate(
            [code[i : i + LANES, :].T[0:1, :] for i in range(0, CHUNK, LANES)], axis=1
        ).astype(I32)
        shift = depth_bins.bit_length() - 1
        col = lax.shift_right_logical(turned, shift) & 255
        row = lax.shift_right_logical(turned, shift + 8)
        col_part = profile(iota((cols_dev, CHUNK), 0) - col + (2 * radius - 1), radius)
        for r in range(rows_dev):
            at = slice(r * cols_dev, (r + 1) * cols_dev)
            row_part = profile((core + CHIP) * rows_dev + r - row + radius, radius)
            row_hi[at, :], row_lo[at, :] = parts_of(col_part * row_part, 2)
        around = (iota((CHUNK, depth_bins), 1) - depth + radius) & (depth_bins - 1)
        col_hi[...], col_lo[...] = parts_of(profile(around, radius) * high, 2)
        added = dot(row_hi[...], col_lo[...]) + dot(row_lo[...], col_hi[...])
        out[...] += added + dot(row_hi[...], col_hi[...])
        return carry

    lax.fori_loop(0, lax.div(total + (CHUNK - 1), CHUNK), one_chunk, 0)
    peak[...] = jnp.full(peak.shape, jnp.max(out[...]), F32)


def spread_max_kernel(recv, out):
    out[...] = jnp.full(out.shape, jnp.max(recv[...]), F32)


def free_kernel(recv, bias, out):
    out[...] = FREE_SCALE * (jnp.max(recv[...]) - bias[...])


def call(body, name, out_shape, *operands, smem=0, space=pltpu.VMEM, scratch=()):
    spaces = [pltpu.SMEM if i < smem else space for i in range(len(operands))]
    operands = [
        x if i < smem else pltpu.with_memory_space_constraint(x, space)
        for i, x in enumerate(operands)
    ]
    out_specs = jax.tree.map(
        lambda s: pl.BlockSpec(
            memory_space=pltpu.SMEM if getattr(s, "dtype", None) == I32 else pltpu.VMEM
        ),
        out_shape,
    )
    return pl.pallas_call(
        body,
        name=name,
        out_shape=out_shape,
        in_specs=[pl.BlockSpec(memory_space=m) for m in spaces],
        out_specs=out_specs,
        scratch_shapes=list(scratch),
        compiler_params=pltpu.CompilerParams(vmem_limit_bytes=24 << 20),
    )(*operands)


def vmem(*dims):
    return pltpu.VMEM(dims, F32)


def hbm(*dims):
    return jax.ShapeDtypeStruct(dims, F32)


def swap(array, axes):
    return lax.all_to_all(array, axes, 0, 0, tiled=True)


def copied(array, axes):
    return swap(jnp.broadcast_to(array[None], (lax.axis_size(axes), *array.shape)), axes)


def per_device(
    bias_grid, hill_slab, hill_row, hill_col, hill_depth, hill_level, hill_count, height_levels
):
    rows_dev, cols_dev, depth_bins = bias_grid.shape
    n_slab = lax.axis_size(SLAB)
    n_walk = lax.axis_size("walk")
    radius = 2 * rows_dev
    grid_cols = cols_dev * n_walk
    senders = n_slab * n_walk
    cells = rows_dev * cols_dev
    chips = n_slab // CHIP
    blocks = senders // LANES
    rows = NEAR * SLOTS

    message, bias = call(
        functools.partial(pack_kernel, rows_dev),
        "pack",
        (vmem(chips, LANES), vmem(cells, depth_bins)),
        hill_count,
        height_levels,
        hill_slab[:, :, 0],
        hill_row,
        hill_col,
        hill_depth,
        hill_level,
        bias_grid.reshape(cells, depth_bins),
        space=pltpu.HBM,
        scratch=[pltpu.SMEM(hill_count.shape, I32), pltpu.SMEM(height_levels.shape, F32)]
        + [pltpu.VMEM(hill_row.shape, I32)] * 5
        + [pltpu.SemaphoreType.DMA((8,))],
    )
    message = swap(message.reshape(chips, 1, LANES), ("y", "z")).reshape(chips, LANES)
    recv = copied(message, CHIP_ROW).reshape(senders, LANES)

    own, table = call(
        functools.partial(height_kernel, cols_dev),
        "heights",
        (vmem(CHIP * n_walk, CHIP * SLOTS, senders), vmem(LANES, senders)),
        recv,
        bias,
        scratch=[pltpu.VMEM((cells, depth_bins), BF16)] * 2
        + [pltpu.VMEM((CHIP * SLOTS, senders), F32)],
    )
    own = swap(own, CHIP_ROW).sum(axis=0)
    ring = range(n_slab)
    below = lax.ppermute(own, SLAB, [(s, (s + CHIP) % n_slab) for s in ring])
    above = lax.ppermute(own, SLAB, [(s, (s - CHIP) % n_slab) for s in ring])

    most = (NEAR - 1) * SLOTS * senders + 8 * NEAR * blocks + UNIT
    most = -(-most // CHUNK) * CHUNK
    codes, place, units = call(
        functools.partial(list_kernel, cols_dev, grid_cols, rows_dev, radius, depth_bins),
        "list",
        (vmem(most, LANES), vmem(rows, senders), jax.ShapeDtypeStruct((2, LANES), I32)),
        table,
        own,
        scratch=[pltpu.VMEM((rows, senders), F32)],
    )
    near, far = ("z", "c"), ("y", "walk")
    n_near, n_far = lax.axis_size(near), lax.axis_size(far)
    new_bias, peak = call(
        functools.partial(deposit_kernel, rows_dev, cols_dev, radius),
        "deposit",
        (vmem(cells, depth_bins), vmem(n_near, LANES)),
        units,
        codes,
        place,
        below,
        own,
        above,
        bias,
        smem=1,
        scratch=[
            pltpu.VMEM((rows, senders), F32),
            pltpu.VMEM((most, LANES), F32),
            pltpu.VMEM((cells, CHUNK), BF16),
            pltpu.VMEM((cells, CHUNK), BF16),
            pltpu.VMEM((CHUNK, depth_bins), BF16),
            pltpu.VMEM((CHUNK, depth_bins), BF16),
        ],
    )
    peaks = swap(peak.reshape(n_near, 1, LANES), near).reshape(n_near, LANES)
    peaks = call(spread_max_kernel, "spread", vmem(n_far, LANES), peaks)
    peaks = swap(peaks.reshape(n_far, 1, LANES), far).reshape(n_far, LANES)
    free = call(free_kernel, "free", hbm(cells, depth_bins), peaks, new_bias)
    return new_bias.reshape(bias_grid.shape), free.reshape(bias_grid.shape)


def solution(mesh):
    split = Mesh(mesh.devices.reshape(8, 8, 2, mesh.shape["walk"]), EVERY)
    in_specs = (
        P(SLAB, "walk", None),
        P(EVERY, None, None),
        P(EVERY, None),
        P(EVERY, None),
        P(EVERY, None),
        P(EVERY, None),
        P(EVERY),
        P(),
    )
    out_specs = (P(SLAB, "walk", None), P(SLAB, "walk", None))
    return jax.shard_map(
        per_device, mesh=split, in_specs=in_specs, out_specs=out_specs, check_vma=False
    )
```

time: 107 us -> 95 us (0.89)
  blocking collectives: 76.2 us -> 60.2 us
  Pallas kernels: 18 us -> 9.97 us
  starting transfers between devices: 5.83 us -> 13.1 us
  waiting for transfers between devices: 5.44 us -> 10.8 us
    all_to_all x4, blocking collectives: 76.2 us -> 60.2 us  [swap(): return lax.all_to_all(array, axes, 0, 0, tiled=True)]
    pallas_call x5 -> x6, Pallas kernels: 18 us -> 9.97 us  [call(): pl.pallas_call(body, name=name, out_shape=out_shape, in_specs=[pl.BlockSp...]
    all_to_all x0 -> x1, starting transfers between devices: none -> 7.8 us  [swap(): return lax.all_to_all(array, axes, 0, 0, tiled=True)]
    all_to_all x0 -> x1, waiting for transfers between devices: none -> 7.56 us  [swap(): return lax.all_to_all(array, axes, 0, 0, tiled=True)]
    ppermute x2, waiting for transfers between devices: 5.44 us -> 3.22 us  [the longest x1 3.22 us: per_device(): below = lax.ppermute(own, SLAB, [(s, (s + CHIP) % n_slab) for s in ring])]
  transfers between devices with their start and end apart: 2 -> 3, of which waited for: 1 -> 2; matrix products, arithmetic and copies ran while one was open for 0% -> 1% of each run, Pallas kernels for 0% -> 2%
where the time goes in v2:
time: 95 us; the launch traced here: 95.8 us
  blocking collectives  60.2 us (63%)
  starting transfers between devices  13.1 us (14%)
  waiting for transfers between devices  10.8 us (11%)
  Pallas kernels  9.97 us (10%)
  local copies, waits for them, and re-layouts  0.99 us (1%)
    all_to_all x4, blocking collectives, swap(): return lax.all_to_all(array, axes, 0, 0, tiled=True)  60.2 us
    pallas_call x6, Pallas kernels, call(): pl.pallas_call(body, name=name, out_shape=out_shape, in_specs=[pl.BlockSp...  9.97 us
    all_to_all x1, starting transfers between devices, swap(): return lax.all_to_all(array, axes, 0, 0, tiled=True)  7.8 us
    all_to_all x1, waiting for transfers between devices, swap(): return lax.all_to_all(array, axes, 0, 0, tiled=True)  7.56 us
    ppermute x1, waiting for transfers between devices, per_device(): below = lax.ppermute(own, SLAB, [(s, (s + CHIP) % n_slab) for s in ring])  3.22 us
    ppermute x1, starting transfers between devices, per_device(): below = lax.ppermute(own, SLAB, [(s, (s + CHIP) % n_slab) for s in ring])  3.09 us
    ppermute x1, starting transfers between devices, per_device(): above = lax.ppermute(own, SLAB, [(s, (s - CHIP) % n_slab) for s in ring])  2.19 us
  transfers between devices with their start and end apart: 3, of which 2 were waited for; matrix products, arithmetic and copies ran while one was open for 1% of the time, Pallas kernels for 2%

profile of v2, /device:TPU:1, one launch (start us, length us, event | category | flops | bytes accessed | tf_op | source)
XLA Modules:
  0.0 95.8 jit_solution(15995714252853372855)
XLA Ops:
  0.6 1.4 %pack.1 = (f32[64,128]{1,0:T(8,128)S(1)}, f32[512,512]{1,0:T(8,128)S(1)}) custom-call(s32[2]{0:T(128)} %refs_0_.1, f32[8]{0:T(128)} %refs_1_.1, s32[2,64]{1,0:T(2,128)} %bitcast.26, s32[2,64]{1,0:T(2,128)} %refs_3_.1, s32[2,64]{1,0:T(2,128)} %refs_4_.1, s32[2,64]{1,0:T(2,128)} %refs_5_.1, s32[2,64]{1,0:T(2,128)} %refs_6_.1, f32[512,512]{1,0:T(8,128)} %bitcast.23), custom_call_target="tpu_custom_call" | custom-call | tf_op jit(solution)/shard_map/pack/pallas_call | solution.py:329
  2.0 27.8 %all_to_all.25 = f32[64,1,128]{2,1,0:T(1,128)S(1)} all-to-all(f32[64,1,128]{2,1,0:T(1,128)S(1)} %bitcast.21), channel_id=1, replica_groups=mesh['y'=8,'z'=8,'c'=2,'walk'=4] {'y','z'}, dimensions={0} | all-to-all | bytes 65536 | tf_op jit(solution)/shard_map/all_to_all | solution.py:349
  29.8 12.7 %all_to_all.26 = f32[8,64,128]{2,1,0:T(8,128)S(1)} all-to-all(f32[8,64,128]{2,1,0:T(8,128)S(1)} %broadcast_in_dim.8), channel_id=1, replica_groups=mesh['y'=8,'z'=8,'c'=2,'walk'=4] {'c','walk'}, dimensions={0} | all-to-all | bytes 524288 | tf_op jit(solution)/shard_map/all_to_all | solution.py:349
  42.5 1.7 %heights.1 = (f32[8,8,512]{2,1,0:T(8,128)S(1)}, f32[128,512]{1,0:T(8,128)S(1)}) custom-call(f32[512,128]{1,0:T(8,128)S(1)} %bitcast.18, f32[512,512]{1,0:T(8,128)S(1)} %get-tuple-element.12.bias), custom_call_target="tpu_custom_call" | custom-call | tf_op jit(solution)/shard_map/heights/pallas_call | solution.py:329
  44.3 8.4 %all_to_all.27 = f32[8,8,512]{2,1,0:T(8,128)S(1)} all-to-all(f32[8,8,512]{2,1,0:T(8,128)S(1)} %get-tuple-element.14), channel_id=1, replica_groups=mesh['y'=8,'z'=8,'c'=2,'walk'=4] {'c','walk'}, dimensions={0} | all-to-all | bytes 262144 | tf_op jit(solution)/shard_map/all_to_all | solution.py:349
  52.7 2.2 %collective-permute-start.1 = (f32[8,512]{1,0:T(8,128)S(1)}, f32[8,512]{1,0:T(8,128)S(1)}, u32[]{:S(2)}, u32[]{:S(2)}) collective-permute-start(f32[8,512]{1,0:T(8,128)S(1)} %reduce_sum.9.after.own), channel_id=1, source_target_pairs={{0,504},{4,508},{8,0},{12,4},{16,8},{20,12},{24,16},{28,20},{32,24... | collective-permute-start | bytes 49160 | tf_op jit(solution)/shard_map/ppermute | solution.py:402
  54.9 3.1 %collective-permute-start = (f32[8,512]{1,0:T(8,128)S(1)}, f32[8,512]{1,0:T(8,128)S(1)}, u32[]{:S(2)}, u32[]{:S(2)}) collective-permute-start(f32[8,512]{1,0:T(8,128)S(1)} %reduce_sum.9.after.own), channel_id=1, source_target_pairs={{0,8},{4,12},{8,16},{12,20},{16,24},{20,28},{24,32},{28,36},{32,40... | collective-permute-start | bytes 49160 | tf_op jit(solution)/shard_map/ppermute | solution.py:401
  58.0 1.5 %list.1 = (f32[10496,128]{1,0:T(8,128)S(1)}, f32[24,512]{1,0:T(8,128)S(1)}, s32[2,128]{1,0:T(2,128)S(1)}) custom-call(f32[128,512]{1,0:T(8,128)S(1)} %get-tuple-element.13.table, f32[8,512]{1,0:T(8,128)S(1)} %reduce_sum.9.after.own), custom_call_target="tpu_custom_call" | custom-call | tf_op jit(solution)/shard_map/list/pallas_call | solution.py:329
  59.5 0.0 collective-permute-done.1.above
  59.5 3.2 %collective-permute-done.below = f32[8,512]{1,0:T(8,128)S(1)} collective-permute-done((f32[8,512]{1,0:T(8,128)S(1)}, f32[8,512]{1,0:T(8,128)S(1)}, u32[]{:S(2)}, u32[]{:S(2)}) %collective-permute-start) | collective-permute-done | bytes 16416 | tf_op jit(solution)/shard_map/ppermute | solution.py:401
  62.7 3.5 %deposit.1 = (f32[512,512]{1,0:T(8,128)S(1)}, f32[16,128]{1,0:T(8,128)S(1)}) custom-call(s32[2,128]{1,0:T(2,128)S(1)} %get-tuple-element.15.units, f32[10496,128]{1,0:T(8,128)S(1)} %get-tuple-element.16.codes, f32[24,512]{1,0:T(8,128)S(1)} %get-tuple-element.17.place, f32[8,512]{1,0:T(8,128)S(1)} %collective-permute-done.below, ...), custom_call_target="tpu_custom_call" | custom-call | tf_op jit(solution)/shard_map/deposit/pallas_call | solution.py:329
  66.2 11.3 %all_to_all.28 = f32[16,1,128]{2,1,0:T(1,128)S(1)} all-to-all(f32[16,1,128]{2,1,0:T(1,128)S(1)} %bitcast.22), channel_id=1, replica_groups=mesh['y'=8,'z'=8,'c'=2,'walk'=4] {'z','c'}, dimensions={0} | all-to-all | bytes 16384 | tf_op jit(solution)/shard_map/all_to_all | solution.py:349
  77.5 0.7 spread.1
  78.2 7.8 %all-to-all-start.4 = ((f32[32,1,128]{2,1,0:T(1,128)}), f32[32,1,128]{2,1,0:T(1,128)S(1)}, u32[]{:S(2)}, u32[]{:S(2)}) async-start(f32[32,1,128]{2,1,0:T(1,128)} %bitcast.11), calls=%async_computation.4 | async-start | bytes 32768 | tf_op jit(solution)/shard_map/all_to_all | solution.py:349
  86.0 1.0 %copy.13 = f32[4,128,512]{2,1,0:T(8,128)} copy(f32[4,128,512]{2,1,0:T(8,128)S(1)} %bitcast.17) | data formatting | bytes 2097152
  87.0 7.6 %all-to-all-done.4 = f32[32,1,128]{2,1,0:T(1,128)S(1)} async-done(((f32[32,1,128]{2,1,0:T(1,128)}), f32[32,1,128]{2,1,0:T(1,128)S(1)}, u32[]{:S(2)}, u32[]{:S(2)}) %all-to-all-start.4) | async-done | bytes 16416 | tf_op jit(solution)/shard_map/all_to_all | solution.py:349
  94.6 1.2 %free.1 = f32[512,512]{1,0:T(8,128)} custom-call(f32[32,128]{1,0:T(8,128)S(1)} %bitcast.19, f32[512,512]{1,0:T(8,128)S(1)} %get-tuple-element.18.bias), custom_call_target="tpu_custom_call" | custom-call | tf_op jit(solution)/shard_map/free/pallas_call | solution.py:329
  (2 shorter events, 0.0 us)
Async XLA Ops:
  52.7 6.8 %collective-permute-start.1 = (f32[8,512]{1,0:T(8,128)S(1)}, f32[8,512]{1,0:T(8,128)S(1)}, u32[]{:S(2)}, u32[]{:S(2)}) collective-permute-start(f32[8,512]{1,0:T(8,128)S(1)} %reduce_sum.9.after.own), channel_id=1, source_target_pairs={{0,504},{4,508},{8,0},{12,4},{16,8},{20,12},{24,16},{28,20},{32,24... | collective-permute-start | bytes 49160 | tf_op jit(solution)/shard_map/ppermute | solution.py:402
  54.9 7.8 %collective-permute-start = (f32[8,512]{1,0:T(8,128)S(1)}, f32[8,512]{1,0:T(8,128)S(1)}, u32[]{:S(2)}, u32[]{:S(2)}) collective-permute-start(f32[8,512]{1,0:T(8,128)S(1)} %reduce_sum.9.after.own), channel_id=1, source_target_pairs={{0,8},{4,12},{8,16},{12,20},{16,24},{20,28},{24,32},{28,36},{32,40... | collective-permute-start | bytes 49160 | tf_op jit(solution)/shard_map/ppermute | solution.py:401
  78.2 16.3 %all-to-all-start.4 = ((f32[32,1,128]{2,1,0:T(1,128)}), f32[32,1,128]{2,1,0:T(1,128)S(1)}, u32[]{:S(2)}, u32[]{:S(2)}) async-start(f32[32,1,128]{2,1,0:T(1,128)} %bitcast.11), calls=%async_computation.4 | async-start | bytes 32768 | tf_op jit(solution)/shard_map/all_to_all | solution.py:349

commit v3 on v2

--- a/solution.py
+++ b/solution.py
@@ -1,4 +1,5 @@
 import functools
+import math
 
 import jax
 import jax.numpy as jnp
@@ -8,8 +9,9 @@
 from jax.sharding import Mesh
 from jax.sharding import PartitionSpec as P
 
-SLAB = ("y", "z", "c")
+SLAB = ("y", "zh", "zl", "c")
 CHIP_ROW = ("c", "walk")
+QUAD = ("zl", "c", "walk")
 EVERY = SLAB + ("walk",)
 
 BASE_HEIGHT = 1.2
@@ -23,8 +25,11 @@
 NEAR = 6
 FIELD = 32
 UNIT = 32
-HELD = 64
+LATER = 64
+HELD = 96
 CHUNK = 256
+STRIPS = 4
+AHEAD = 4
 
 F32 = jnp.float32
 BF16 = jnp.bfloat16
@@ -189,6 +194,7 @@
 
     lax.fori_loop(0, lax.div(most + (HELD - 1), HELD), one_pass, 0)
     height = jnp.where(held, base * jnp.exp(-found[...] / TEMPER), 0.0)
+    height = height[:SLOTS, :] + height[SLOTS:, :]
     for i in range(out.shape[0]):
         out[i] = height
 
@@ -197,25 +203,29 @@
     for u in range(units):
 
         def later(t, carry, u=u):
-            write(u, t, pl.multiple_of(offset[u] + t * UNIT, 8))
+            first = UNIT + t * LATER
+            write(u, first, LATER, offset[u] + first)
             return carry
 
-        lax.fori_loop(1, lax.div(count[u] + (UNIT - 1), UNIT), later, 0)
+        lax.fori_loop(0, lax.div(count[u] + (LATER - 1 - UNIT), LATER), later, 0)
     for u in range(units):
-        write(u, 0, pl.multiple_of(offset[u], 8))
-
-
-def gathered(place, field, u, blocks, t):
-    number = (iota((UNIT, LANES), 0) + t * UNIT).astype(F32)
+        write(u, 0, UNIT, offset[u])
+
+
+def gathered(place, field, u, blocks, first, rows):
+    number = (iota((rows, LANES), 0) + first).astype(F32)
     q, j = u // blocks, u % blocks
     at = slice(j * LANES, (j + 1) * LANES)
-    found = jnp.zeros((UNIT, LANES), F32)
+    found = jnp.zeros((rows, LANES), F32)
     for i in range(q * SLOTS, (q + 1) * SLOTS):
         found = jnp.where(place[i : i + 1, at] == number, field[i : i + 1, at], found)
-    return jnp.broadcast_to(jnp.sum(found, axis=1, keepdims=True), (UNIT, LANES))
-
-
-def list_kernel(cols_dev, grid_cols, rows_dev, radius, depth_bins, table, after, codes, place, units, code):
+    return jnp.broadcast_to(jnp.sum(found, axis=1, keepdims=True), (rows, LANES))
+
+
+def list_kernel(
+    cols_dev, grid_cols, rows_dev, radius, depth_bins,
+    table, after, codes, place, units, planes, lines, code,
+):
     senders = table.shape[1]
     blocks = senders // LANES
     rows = NEAR * SLOTS
@@ -229,8 +239,8 @@
     col = (col - walk * cols_dev + (radius - 1)) & (grid_cols - 1)
     near = lax.shift_right_logical(line, 2)
     reached = (near >= core) & (near < core + NEAR - 1) & (col < cols_dev + 2 * radius - 1)
-    active = reached & (base != 0.0)
     row = near * rows_dev + (row & (rows_dev - 1))
+    active = reached & (base != 0.0) & (row > core * rows_dev)
     code[...] = ((row * 256 + col) * depth_bins + depth).astype(F32)
     places, counts = numbered(active.astype(F32))
     for j in range(blocks):
@@ -242,76 +252,123 @@
         n = jnp.max(counts[u % blocks][i : i + 1, :]).astype(I32)
         units[0, u] = total
         units[1, u] = n
-        total = total + ((n + 7) & -8)
+        total = total + n
     units[0, n_units] = total
 
-    def write(u, t, row):
-        codes[pl.ds(row, UNIT), :] = gathered(place, code, u, blocks, t)
+    def write(u, first, size, row):
+        codes[pl.ds(row, size), :] = gathered(place, code, u, blocks, first, size)
 
     in_windows(n_units, units.at[0], units.at[1], write)
 
-
-def profile(shifted, radius):
+    def ahead(g, carry):
+        listed = live_rows(codes, pl.multiple_of(g * CHUNK, CHUNK), total)
+        factors(
+            listed, core, rows_dev, cols_dev, depth_bins, radius, planes.at[g], lines.at[g]
+        )
+        return carry
+
+    lax.fori_loop(0, jnp.minimum(chunks_of(total), AHEAD), ahead, 0)
+
+
+def profile(shifted, radius, wrapped=False):
     spread = SIGMA_SHARE * radius
-    t = (shifted - radius).astype(F32)
-    within = (shifted >= 0) & (shifted < 2 * radius)
-    return jnp.where(within, jnp.exp(-(t * t) / (2.0 * spread * spread)), 0.0)
+    t = shifted.astype(F32) - radius
+    within = shifted < 2 * radius
+    if not wrapped:
+        within = within & (shifted >= 0)
+    return jnp.where(within, jnp.exp2(t * t * (-math.log2(math.e) / (2.0 * spread**2))), 0.0)
+
+
+def factors(code, core, rows_dev, cols_dev, depth_bins, radius, planes, lines):
+    depth = code[:, 0:1].astype(I32) & (depth_bins - 1)
+    around = (iota((CHUNK, depth_bins), 1) + (radius - depth)) & (depth_bins - 1)
+    lines[...] = profile(around, radius, wrapped=True)
+    turned = jnp.concatenate(
+        [code[i : i + LANES, :].T[0:1, :] for i in range(0, CHUNK, LANES)], axis=1
+    ).astype(I32)
+    shift = depth_bins.bit_length() - 1
+    col = lax.shift_right_logical(turned, shift) & 255
+    row = lax.shift_right_logical(turned, shift + 8)
+    col_part = profile(iota((cols_dev, CHUNK), 0) - col + (2 * radius - 1), radius)
+    for r in range(rows_dev):
+        at = slice(r * cols_dev, (r + 1) * cols_dev)
+        row_part = profile((core + CHIP) * rows_dev + r - row + radius, radius)
+        hi, lo = parts_of(col_part * row_part, 2)
+        planes[at, 0:CHUNK] = hi
+        planes[at, CHUNK : 2 * CHUNK] = hi
+        planes[at, 2 * CHUNK : 3 * CHUNK] = lo
+
+
+def live_rows(array, start, total):
+    live = iota((CHUNK, LANES), 0) + start < total
+    return jnp.where(live, array[pl.ds(start, CHUNK), :], 0.0)
+
+
+def chunks_of(total):
+    return lax.div(total + (CHUNK - 1), CHUNK)
 
 
 def deposit_kernel(
     rows_dev, cols_dev, radius,
-    units, codes, place, below, own, above, bias, out, peak,
-    heights, height, row_hi, row_lo, col_hi, col_lo,
+    units, codes, place, planes, lines, quad, edge, bias, out, peak,
+    heights, height, more_planes, more_lines, scaled,
 ):
     blocks = place.shape[1] // LANES
-    cells, depth_bins = bias.shape
+    depth_bins = bias.shape[1]
     core = lax.axis_index("c")
-    rows = CHIP * SLOTS
-    heights[0:rows, :] = below[...]
-    heights[rows : 2 * rows, :] = own[...]
-    heights[2 * rows : 3 * rows, :] = above[...]
+    lower = lax.axis_index("zl") == 0
+    for k in range(CHIP):
+        parts = edge[CHIP + k], quad[k], quad[CHIP + k], edge[k]
+        for i in range(NEAR // CHIP):
+            at = (i * CHIP + k) * SLOTS
+            heights[at : at + SLOTS, :] = jnp.where(lower, parts[i], parts[i + 1])
     n_units = NEAR * blocks
 
-    def write(u, t, row):
-        height[pl.ds(row, UNIT), :] = gathered(place, heights, u, blocks, t)
+    def write(u, first, size, row):
+        height[pl.ds(row, size), :] = gathered(place, heights, u, blocks, first, size)
 
     in_windows(n_units, units.at[0], units.at[1], write)
     total = units[0, n_units]
     out[...] = bias[...]
 
-    def one_chunk(g, carry):
-        start = pl.multiple_of(g * CHUNK, CHUNK)
-        live = iota((CHUNK, LANES), 0) + start < total
-        code = jnp.where(live, codes[pl.ds(start, CHUNK), :], 0.0)
-        high = jnp.where(live, height[pl.ds(start, CHUNK), :], 0.0)[:, 0:1]
-        depth = code[:, 0:1].astype(I32) & (depth_bins - 1)
-        turned = jnp.concatenate(
-            [code[i : i + LANES, :].T[0:1, :] for i in range(0, CHUNK, LANES)], axis=1
-        ).astype(I32)
-        shift = depth_bins.bit_length() - 1
-        col = lax.shift_right_logical(turned, shift) & 255
-        row = lax.shift_right_logical(turned, shift + 8)
-        col_part = profile(iota((cols_dev, CHUNK), 0) - col + (2 * radius - 1), radius)
-        for r in range(rows_dev):
-            at = slice(r * cols_dev, (r + 1) * cols_dev)
-            row_part = profile((core + CHIP) * rows_dev + r - row + radius, radius)
-            row_hi[at, :], row_lo[at, :] = parts_of(col_part * row_part, 2)
-        around = (iota((CHUNK, depth_bins), 1) - depth + radius) & (depth_bins - 1)
-        col_hi[...], col_lo[...] = parts_of(profile(around, radius) * high, 2)
-        added = dot(row_hi[...], col_lo[...]) + dot(row_lo[...], col_hi[...])
-        out[...] += added + dot(row_hi[...], col_hi[...])
+    def add(g, plane, line):
+        high = live_rows(height, pl.multiple_of(g * CHUNK, CHUNK), total)[:, 0:1]
+        hi, lo = parts_of(line * high, 2)
+        scaled[0:CHUNK, :] = hi
+        scaled[CHUNK : 2 * CHUNK, :] = lo
+        scaled[2 * CHUNK : 3 * CHUNK, :] = hi
+        out[...] += dot(plane, scaled[...])
+
+    def ready(g, carry):
+        add(g, planes[g], lines[g])
         return carry
 
-    lax.fori_loop(0, lax.div(total + (CHUNK - 1), CHUNK), one_chunk, 0)
+    def rest(g, carry):
+        code = live_rows(codes, pl.multiple_of(g * CHUNK, CHUNK), total)
+        factors(code, core, rows_dev, cols_dev, depth_bins, radius, more_planes, more_lines)
+        add(g, more_planes[...], more_lines[...])
+        return carry
+
+    count = chunks_of(total)
+    lax.fori_loop(0, jnp.minimum(count, AHEAD), ready, 0)
+    lax.fori_loop(AHEAD, count, rest, 0)
     peak[...] = jnp.full(peak.shape, jnp.max(out[...]), F32)
 
 
-def spread_max_kernel(recv, out):
-    out[...] = jnp.full(out.shape, jnp.max(recv[...]), F32)
-
-
-def free_kernel(recv, bias, out):
-    out[...] = FREE_SCALE * (jnp.max(recv[...]) - bias[...])
+def free_kernel(recv, bias, bias_out, out, free, sems):
+    bias_copy = pltpu.make_async_copy(bias, bias_out, sems.at[STRIPS])
+    bias_copy.start()
+    highest = jnp.max(recv[...])
+    size = bias.shape[0] // STRIPS
+    copies = []
+    for i in range(STRIPS):
+        at = pl.ds(i * size, size)
+        free[at, :] = FREE_SCALE * (highest - bias[at, :])
+        copies.append(pltpu.make_async_copy(free.at[at, :], out.at[at, :], sems.at[i]))
+        copies[-1].start()
+    for c in copies:
+        c.wait()
+    bias_copy.wait()
 
 
 def call(body, name, out_shape, *operands, smem=0, space=pltpu.VMEM, scratch=()):
@@ -320,12 +377,12 @@
         x if i < smem else pltpu.with_memory_space_constraint(x, space)
         for i, x in enumerate(operands)
     ]
-    out_specs = jax.tree.map(
-        lambda s: pl.BlockSpec(
-            memory_space=pltpu.SMEM if getattr(s, "dtype", None) == I32 else pltpu.VMEM
-        ),
-        out_shape,
-    )
+    def space_of(shape):
+        if isinstance(shape, jax.ShapeDtypeStruct):
+            return pltpu.SMEM if shape.dtype == I32 else pltpu.HBM
+        return pltpu.VMEM
+
+    out_specs = jax.tree.map(lambda s: pl.BlockSpec(memory_space=space_of(s)), out_shape)
     return pl.pallas_call(
         body,
         name=name,
@@ -366,6 +423,7 @@
     chips = n_slab // CHIP
     blocks = senders // LANES
     rows = NEAR * SLOTS
+    quads = 2 * CHIP
 
     message, bias = call(
         functools.partial(pack_kernel, rows_dev),
@@ -384,34 +442,39 @@
         + [pltpu.VMEM(hill_row.shape, I32)] * 5
         + [pltpu.SemaphoreType.DMA((8,))],
     )
-    message = swap(message.reshape(chips, 1, LANES), ("y", "z")).reshape(chips, LANES)
+    message = swap(message.reshape(chips, 1, LANES), ("y", "zh", "zl")).reshape(chips, LANES)
     recv = copied(message, CHIP_ROW).reshape(senders, LANES)
 
     own, table = call(
         functools.partial(height_kernel, cols_dev),
         "heights",
-        (vmem(CHIP * n_walk, CHIP * SLOTS, senders), vmem(LANES, senders)),
+        (vmem(quads * n_walk, SLOTS, senders), vmem(LANES, senders)),
         recv,
         bias,
         scratch=[pltpu.VMEM((cells, depth_bins), BF16)] * 2
         + [pltpu.VMEM((CHIP * SLOTS, senders), F32)],
     )
-    own = swap(own, CHIP_ROW).sum(axis=0)
-    ring = range(n_slab)
-    below = lax.ppermute(own, SLAB, [(s, (s + CHIP) % n_slab) for s in ring])
-    above = lax.ppermute(own, SLAB, [(s, (s - CHIP) % n_slab) for s in ring])
-
-    most = (NEAR - 1) * SLOTS * senders + 8 * NEAR * blocks + UNIT
+    quad = swap(own, QUAD).reshape(quads, n_walk, SLOTS, senders).sum(axis=1)
+    route = [(s, (s + (CHIP if s % quads >= CHIP else -CHIP)) % n_slab) for s in range(n_slab)]
+    edge = lax.ppermute(quad, SLAB, route)
+
+    most = (NEAR - 1) * SLOTS * senders + LATER
     most = -(-most // CHUNK) * CHUNK
-    codes, place, units = call(
+    codes, place, units, planes, lines = call(
         functools.partial(list_kernel, cols_dev, grid_cols, rows_dev, radius, depth_bins),
         "list",
-        (vmem(most, LANES), vmem(rows, senders), jax.ShapeDtypeStruct((2, LANES), I32)),
+        (
+            vmem(most, LANES),
+            vmem(rows, senders),
+            jax.ShapeDtypeStruct((2, LANES), I32),
+            pltpu.VMEM((AHEAD, cells, 3 * CHUNK), BF16),
+            vmem(AHEAD, CHUNK, depth_bins),
+        ),
         table,
-        own,
+        quad,
         scratch=[pltpu.VMEM((rows, senders), F32)],
     )
-    near, far = ("z", "c"), ("y", "walk")
+    near, far = ("zh", "zl", "c"), ("y", "walk")
     n_near, n_far = lax.axis_size(near), lax.axis_size(far)
     new_bias, peak = call(
         functools.partial(deposit_kernel, rows_dev, cols_dev, radius),
@@ -420,29 +483,38 @@
         units,
         codes,
         place,
-        below,
-        own,
-        above,
+        planes,
+        lines,
+        quad,
+        edge,
         bias,
         smem=1,
         scratch=[
             pltpu.VMEM((rows, senders), F32),
             pltpu.VMEM((most, LANES), F32),
-            pltpu.VMEM((cells, CHUNK), BF16),
-            pltpu.VMEM((cells, CHUNK), BF16),
-            pltpu.VMEM((CHUNK, depth_bins), BF16),
-            pltpu.VMEM((CHUNK, depth_bins), BF16),
+            pltpu.VMEM((cells, 3 * CHUNK), BF16),
+            pltpu.VMEM((CHUNK, depth_bins), F32),
+            pltpu.VMEM((3 * CHUNK, depth_bins), BF16),
         ],
     )
-    peaks = swap(peak.reshape(n_near, 1, LANES), near).reshape(n_near, LANES)
-    peaks = call(spread_max_kernel, "spread", vmem(n_far, LANES), peaks)
-    peaks = swap(peaks.reshape(n_far, 1, LANES), far).reshape(n_far, LANES)
-    free = call(free_kernel, "free", hbm(cells, depth_bins), peaks, new_bias)
+    peaks = swap(peak.reshape(n_near, 1, LANES), near).max(axis=0)
+    peaks = swap(jnp.broadcast_to(peaks, (n_far, 1, LANES)), far).reshape(n_far, LANES)
+    new_bias, free = call(
+        free_kernel,
+        "free",
+        (hbm(cells, depth_bins), hbm(cells, depth_bins)),
+        peaks,
+        new_bias,
+        scratch=[
+            pltpu.VMEM((cells, depth_bins), F32),
+            pltpu.SemaphoreType.DMA((STRIPS + 1,)),
+        ],
+    )
     return new_bias.reshape(bias_grid.shape), free.reshape(bias_grid.shape)
 
 
 def solution(mesh):
-    split = Mesh(mesh.devices.reshape(8, 8, 2, mesh.shape["walk"]), EVERY)
+    split = Mesh(mesh.devices.reshape(8, 4, 2, 2, mesh.shape["walk"]), EVERY)
     in_specs = (
         P(SLAB, "walk", None),
         P(EVERY, None, None),

time: 95 us -> 89.4 us (0.941); the launches traced: 95.8 us -> 88.9 us
  blocking collectives: 60.2 us -> 72.5 us
  starting transfers between devices: 13.1 us -> 2.41 us
  waiting for transfers between devices: 10.8 us -> 2.96 us
  local copies, waits for them, and re-layouts: 0.99 us -> 0.03 us
    all_to_all x4 -> x5, blocking collectives: 60.2 us -> 72.5 us  [swap(): return lax.all_to_all(array, axes, 0, 0, tiled=True)]
    all_to_all x1 -> x0, starting transfers between devices: 7.8 us -> none  [swap(): return lax.all_to_all(array, axes, 0, 0, tiled=True)]
    all_to_all x1 -> x0, waiting for transfers between devices: 7.56 us -> none  [swap(): return lax.all_to_all(array, axes, 0, 0, tiled=True)]
    ppermute x2 -> x1, starting transfers between devices: 5.28 us -> 2.41 us  [per_device(): edge = lax.ppermute(quad, SLAB, route)]
    unnamed x1 -> x0, local copies, waits for them, and re-layouts: 0.97 us -> none
    pallas_call x6 -> x5, Pallas kernels: 9.97 us -> 10.3 us  [call(): pl.pallas_call(body, name=name, out_shape=out_shape, in_specs=[pl.BlockSp...]
    ppermute x2 -> x1, waiting for transfers between devices: 3.22 us -> 2.96 us  [per_device(): edge = lax.ppermute(quad, SLAB, route)]
  transfers between devices with their start and end apart: 3 -> 1, of which waited for: 2 -> 1; matrix products, arithmetic and copies ran while one was open for 1% -> 0% of each run, Pallas kernels for 2% -> 3%
where the time goes in v3:
time: 89.4 us; the launch traced here: 88.9 us
  blocking collectives  72.5 us (81%)
  Pallas kernels  10.3 us (12%)
  waiting for transfers between devices  2.96 us (3%)
  starting transfers between devices  2.41 us (3%)
    all_to_all x5, blocking collectives, swap(): return lax.all_to_all(array, axes, 0, 0, tiled=True)  72.5 us
    pallas_call x5, Pallas kernels, call(): pl.pallas_call(body, name=name, out_shape=out_shape, in_specs=[pl.BlockSp...  10.3 us
    ppermute x1, waiting for transfers between devices, per_device(): edge = lax.ppermute(quad, SLAB, route)  2.96 us
    ppermute x1, starting transfers between devices, per_device(): edge = lax.ppermute(quad, SLAB, route)  2.41 us
  transfers between devices with their start and end apart: 1, of which 1 were waited for; matrix products, arithmetic and copies ran while one was open for 0% of the time, Pallas kernels for 3%

profile of v3, /device:TPU:1, one launch (start us, length us, event | category | flops | bytes accessed | tf_op | source)
XLA Modules:
  0.0 88.9 jit_solution(13194838135511040102)
XLA Ops:
  0.6 1.4 %pack.1 = (f32[64,128]{1,0:T(8,128)S(1)}, f32[512,512]{1,0:T(8,128)S(1)}) custom-call(s32[2]{0:T(128)} %refs_0_.1, f32[8]{0:T(128)} %refs_1_.1, s32[2,64]{1,0:T(2,128)} %bitcast.21, s32[2,64]{1,0:T(2,128)} %refs_3_.1, s32[2,64]{1,0:T(2,128)} %refs_4_.1, s32[2,64]{1,0:T(2,128)} %refs_5_.1, s32[2,64]{1,0:T(2,128)} %refs_6_.1, f32[512,512]{1,0:T(8,128)} %bitcast.19), custom_call_target="tpu_custom_call" | custom-call | tf_op jit(solution)/shard_map/pack/pallas_call | solution.py:386
  2.0 27.8 %all_to_all.25 = f32[64,1,128]{2,1,0:T(1,128)S(1)} all-to-all(f32[64,1,128]{2,1,0:T(1,128)S(1)} %bitcast.17), channel_id=1, replica_groups=mesh['y'=8,'zh'=4,'zl'=2,'c'=2,'walk'=4] {'y','zh','zl'}, dimensions={0} | all-to-all | bytes 65536 | tf_op jit(solution)/shard_map/all_to_all | solution.py:406
  29.8 12.7 %all_to_all.26 = f32[8,64,128]{2,1,0:T(8,128)S(1)} all-to-all(f32[8,64,128]{2,1,0:T(8,128)S(1)} %broadcast_in_dim.11), channel_id=1, replica_groups=mesh['y'=8,'zh'=4,'zl'=2,'c'=2,'walk'=4] {'c','walk'}, dimensions={0} | all-to-all | bytes 524288 | tf_op jit(solution)/shard_map/all_to_all | solution.py:406
  42.5 1.9 %heights.1 = (f32[16,4,512]{2,1,0:T(4,128)S(1)}, f32[128,512]{1,0:T(8,128)S(1)}) custom-call(f32[512,128]{1,0:T(8,128)S(1)} %bitcast.15, f32[512,512]{1,0:T(8,128)S(1)} %get-tuple-element.16.bias), custom_call_target="tpu_custom_call" | custom-call | tf_op jit(solution)/shard_map/heights/pallas_call | solution.py:386
  44.5 9.3 %all_to_all.27 = f32[16,4,512]{2,1,0:T(4,128)S(1)} all-to-all(f32[16,4,512]{2,1,0:T(4,128)S(1)} %get-tuple-element.18), channel_id=1, replica_groups=mesh['y'=8,'zh'=4,'zl'=2,'c'=2,'walk'=4] {'zl','c','walk'}, dimensions={0} | all-to-all | bytes 262144 | tf_op jit(solution)/shard_map/all_to_all | solution.py:406
  53.8 2.4 %collective-permute-start = (f32[4,4,512]{2,1,0:T(4,128)S(1)}, f32[4,4,512]{2,1,0:T(4,128)S(1)}, u32[]{:S(2)}, u32[]{:S(2)}) collective-permute-start(f32[4,4,512]{2,1,0:T(4,128)S(1)} %bitcast_reduce_fusion.after.quad), channel_id=1, source_target_pairs={{0,504},{4,508},{8,16},{12,20},{16,8},{20,12},{24,32},{28,36},{32,... | collective-permute-start | bytes 98312 | tf_op jit(solution)/shard_map/ppermute | solution.py:459
  56.3 2.6 %list.1 = (f32[10496,128]{1,0:T(8,128)S(1)}, f32[24,512]{1,0:T(8,128)S(1)}, s32[2,128]{1,0:T(2,128)S(1)}, bf16[4,512,768]{2,1,0:T(8,128)(2,1)S(1)}, f32[4,256,512]{2,1,0:T(8,128)S(1)}) custom-call(f32[128,512]{1,0:T(8,128)S(1)} %get-tuple-element.17.table, f32[4,4,512]{2,1,0:T(4,128)S(1)} %bitcast_reduce_fusion.after.quad), custom_call_target="tpu_custom_call" | custom-call | tf_op jit(solution)/shard_map/list/pallas_call | solution.py:386
  58.9 3.0 %collective-permute-done.edge = f32[4,4,512]{2,1,0:T(4,128)S(1)} collective-permute-done((f32[4,4,512]{2,1,0:T(4,128)S(1)}, f32[4,4,512]{2,1,0:T(4,128)S(1)}, u32[]{:S(2)}, u32[]{:S(2)}) %collective-permute-start) | collective-permute-done | bytes 32800 | tf_op jit(solution)/shard_map/ppermute | solution.py:459
  61.8 3.1 %deposit.1 = (f32[512,512]{1,0:T(8,128)S(1)}, f32[16,128]{1,0:T(8,128)S(1)}) custom-call(s32[2,128]{1,0:T(2,128)S(1)} %get-tuple-element.19.units, f32[10496,128]{1,0:T(8,128)S(1)} %get-tuple-element.20.codes, f32[24,512]{1,0:T(8,128)S(1)} %get-tuple-element.21.place, bf16[4,512,768]{2,1,0:T(8,128)(2,1)S(1)} %get-tuple-element.22.planes, ...), custom_call_target="tpu_custom_call" | custom-call | tf_op jit(solution)/shard_map/deposit/pallas_call | solution.py:386
  64.9 11.1 %all_to_all.28 = f32[16,1,128]{2,1,0:T(1,128)S(1)} all-to-all(f32[16,1,128]{2,1,0:T(1,128)S(1)} %bitcast.18), channel_id=1, replica_groups=mesh['y'=8,'zh'=4,'zl'=2,'c'=2,'walk'=4] {'zh','zl','c'}, dimensions={0} | all-to-all | bytes 16384 | tf_op jit(solution)/shard_map/all_to_all | solution.py:406
  76.0 11.6 %all_to_all.29 = f32[32,1,128]{2,1,0:T(1,128)S(1)} all-to-all(f32[32,1,128]{2,1,0:T(1,128)S(1)} %broadcast_in_dim.12), channel_id=1, replica_groups=mesh['y'=8,'zh'=4,'zl'=2,'c'=2,'walk'=4] {'y','walk'}, dimensions={0} | all-to-all | bytes 32768 | tf_op jit(solution)/shard_map/all_to_all | solution.py:406
  87.6 1.4 %free.1 = (f32[512,512]{1,0:T(8,128)}, f32[512,512]{1,0:T(8,128)}) custom-call(f32[32,128]{1,0:T(8,128)S(1)} %bitcast.16, f32[512,512]{1,0:T(8,128)S(1)} %get-tuple-element.25.bias), custom_call_target="tpu_custom_call" | custom-call | tf_op jit(solution)/shard_map/free/pallas_call | solution.py:386
  (4 shorter events, 0.1 us)
Async XLA Ops:
  53.8 8.0 %collective-permute-start = (f32[4,4,512]{2,1,0:T(4,128)S(1)}, f32[4,4,512]{2,1,0:T(4,128)S(1)}, u32[]{:S(2)}, u32[]{:S(2)}) collective-permute-start(f32[4,4,512]{2,1,0:T(4,128)S(1)} %bitcast_reduce_fusion.after.quad), channel_id=1, source_target_pairs={{0,504},{4,508},{8,16},{12,20},{16,8},{20,12},{24,32},{28,36},{32,... | collective-permute-start | bytes 98312 | tf_op jit(solution)/shard_map/ppermute | solution.py:459

commit v4 on v3

--- a/solution.py
+++ b/solution.py
@@ -199,15 +199,24 @@
         out[i] = height
 
 
-def in_windows(units, offset, count, write):
-    for u in range(units):
-
-        def later(t, carry, u=u):
-            first = UNIT + t * LATER
-            write(u, first, LATER, offset[u] + first)
-            return carry
-
-        lax.fori_loop(0, lax.div(count[u] + (LATER - 1 - UNIT), LATER), later, 0)
+def in_windows(blocks, offset, count, write):
+    units = NEAR * blocks
+
+    @pl.when(count[units] > UNIT)
+    def _():
+        for q in range(NEAR):
+            some = range(q * blocks, (q + 1) * blocks)
+            most = functools.reduce(jnp.maximum, [count[u] for u in some])
+            times = lax.div(most + (LATER - 1 - UNIT), LATER)
+
+            def later(t, carry, some=some, times=times):
+                first = UNIT + (times - 1 - t) * LATER
+                for u in some:
+                    write(u, first, LATER, offset[u] + first)
+                return carry
+
+            lax.fori_loop(0, times, later, 0)
+
     for u in range(units):
         write(u, 0, UNIT, offset[u])
 
@@ -245,7 +254,7 @@
     places, counts = numbered(active.astype(F32))
     for j in range(blocks):
         place[:, j * LANES : (j + 1) * LANES] = places[j]
-    total = jnp.int32(0)
+    total, most = jnp.int32(0), jnp.int32(0)
     n_units = NEAR * blocks
     for u in range(n_units):
         i = (u // blocks) * SLOTS + SLOTS - 1
@@ -253,12 +262,14 @@
         units[0, u] = total
         units[1, u] = n
         total = total + n
+        most = jnp.maximum(most, n)
     units[0, n_units] = total
+    units[1, n_units] = most
 
     def write(u, first, size, row):
         codes[pl.ds(row, size), :] = gathered(place, code, u, blocks, first, size)
 
-    in_windows(n_units, units.at[0], units.at[1], write)
+    in_windows(blocks, units.at[0], units.at[1], write)
 
     def ahead(g, carry):
         listed = live_rows(codes, pl.multiple_of(g * CHUNK, CHUNK), total)
@@ -327,17 +338,21 @@
     def write(u, first, size, row):
         height[pl.ds(row, size), :] = gathered(place, heights, u, blocks, first, size)
 
-    in_windows(n_units, units.at[0], units.at[1], write)
+    in_windows(blocks, units.at[0], units.at[1], write)
     total = units[0, n_units]
-    out[...] = bias[...]
-
-    def add(g, plane, line):
+    count = chunks_of(total)
+
+    @pl.when(count == 0)
+    def _():
+        out[...] = bias[...]
+
+    def add(g, plane, line, start=out):
         high = live_rows(height, pl.multiple_of(g * CHUNK, CHUNK), total)[:, 0:1]
         hi, lo = parts_of(line * high, 2)
         scaled[0:CHUNK, :] = hi
         scaled[CHUNK : 2 * CHUNK, :] = lo
         scaled[2 * CHUNK : 3 * CHUNK, :] = hi
-        out[...] += dot(plane, scaled[...])
+        out[...] = start[...] + dot(plane, scaled[...])
 
     def ready(g, carry):
         add(g, planes[g], lines[g])
@@ -349,8 +364,11 @@
         add(g, more_planes[...], more_lines[...])
         return carry
 
-    count = chunks_of(total)
-    lax.fori_loop(0, jnp.minimum(count, AHEAD), ready, 0)
+    @pl.when(count > 0)
+    def _():
+        add(0, planes[0], lines[0], bias)
+
+    lax.fori_loop(1, jnp.minimum(count, AHEAD), ready, 0)
     lax.fori_loop(AHEAD, count, rest, 0)
     peak[...] = jnp.full(peak.shape, jnp.max(out[...]), F32)
 
@@ -458,7 +476,7 @@
     route = [(s, (s + (CHIP if s % quads >= CHIP else -CHIP)) % n_slab) for s in range(n_slab)]
     edge = lax.ppermute(quad, SLAB, route)
 
-    most = (NEAR - 1) * SLOTS * senders + LATER
+    most = (NEAR - 1) * SLOTS * senders + UNIT + SLOTS * LANES + LATER
     most = -(-most // CHUNK) * CHUNK
     codes, place, units, planes, lines = call(
         functools.partial(list_kernel, cols_dev, grid_cols, rows_dev, radius, depth_bins),

time: 89.4 us -> 88.9 us (level)
  no operation moved by 1% of the time
where the time goes in v4:
time: 88.9 us; the launch traced here: 88.7 us
  blocking collectives  72.6 us (82%)
  Pallas kernels  9.7 us (11%)
  waiting for transfers between devices  3.26 us (4%)
  starting transfers between devices  2.41 us (3%)
    all_to_all x5, blocking collectives, swap(): return lax.all_to_all(array, axes, 0, 0, tiled=True)  72.6 us
    pallas_call x5, Pallas kernels, call(): pl.pallas_call(body, name=name, out_shape=out_shape, in_specs=[pl.BlockSp...  9.7 us
    ppermute x1, waiting for transfers between devices, per_device(): edge = lax.ppermute(quad, SLAB, route)  3.26 us
    ppermute x1, starting transfers between devices, per_device(): edge = lax.ppermute(quad, SLAB, route)  2.41 us
  transfers between devices with their start and end apart: 1, of which 1 were waited for; matrix products, arithmetic and copies ran while one was open for 0% of the time, Pallas kernels for 3%

profile of v4, /device:TPU:1, one launch (start us, length us, event | category | flops | bytes accessed | tf_op | source)
XLA Modules:
  0.0 88.7 jit_solution(14858376824503777930)
XLA Ops:
  0.6 1.4 %pack.1 = (f32[64,128]{1,0:T(8,128)S(1)}, f32[512,512]{1,0:T(8,128)S(1)}) custom-call(s32[2]{0:T(128)} %refs_0_.1, f32[8]{0:T(128)} %refs_1_.1, s32[2,64]{1,0:T(2,128)} %bitcast.21, s32[2,64]{1,0:T(2,128)} %refs_3_.1, s32[2,64]{1,0:T(2,128)} %refs_4_.1, s32[2,64]{1,0:T(2,128)} %refs_5_.1, s32[2,64]{1,0:T(2,128)} %refs_6_.1, f32[512,512]{1,0:T(8,128)} %bitcast.19), custom_call_target="tpu_custom_call" | custom-call | tf_op jit(solution)/shard_map/pack/pallas_call | solution.py:404
  2.0 27.8 %all_to_all.25 = f32[64,1,128]{2,1,0:T(1,128)S(1)} all-to-all(f32[64,1,128]{2,1,0:T(1,128)S(1)} %bitcast.17), channel_id=1, replica_groups=mesh['y'=8,'zh'=4,'zl'=2,'c'=2,'walk'=4] {'y','zh','zl'}, dimensions={0} | all-to-all | bytes 65536 | tf_op jit(solution)/shard_map/all_to_all | solution.py:424
  29.8 12.7 %all_to_all.26 = f32[8,64,128]{2,1,0:T(8,128)S(1)} all-to-all(f32[8,64,128]{2,1,0:T(8,128)S(1)} %broadcast_in_dim.11), channel_id=1, replica_groups=mesh['y'=8,'zh'=4,'zl'=2,'c'=2,'walk'=4] {'c','walk'}, dimensions={0} | all-to-all | bytes 524288 | tf_op jit(solution)/shard_map/all_to_all | solution.py:424
  42.5 1.9 %heights.1 = (f32[16,4,512]{2,1,0:T(4,128)S(1)}, f32[128,512]{1,0:T(8,128)S(1)}) custom-call(f32[512,128]{1,0:T(8,128)S(1)} %bitcast.15, f32[512,512]{1,0:T(8,128)S(1)} %get-tuple-element.16.bias), custom_call_target="tpu_custom_call" | custom-call | tf_op jit(solution)/shard_map/heights/pallas_call | solution.py:404
  44.5 9.3 %all_to_all.27 = f32[16,4,512]{2,1,0:T(4,128)S(1)} all-to-all(f32[16,4,512]{2,1,0:T(4,128)S(1)} %get-tuple-element.18), channel_id=1, replica_groups=mesh['y'=8,'zh'=4,'zl'=2,'c'=2,'walk'=4] {'zl','c','walk'}, dimensions={0} | all-to-all | bytes 262144 | tf_op jit(solution)/shard_map/all_to_all | solution.py:424
  53.8 2.4 %collective-permute-start = (f32[4,4,512]{2,1,0:T(4,128)S(1)}, f32[4,4,512]{2,1,0:T(4,128)S(1)}, u32[]{:S(2)}, u32[]{:S(2)}) collective-permute-start(f32[4,4,512]{2,1,0:T(4,128)S(1)} %bitcast_reduce_fusion.after.quad), channel_id=1, source_target_pairs={{0,504},{4,508},{8,16},{12,20},{16,8},{20,12},{24,32},{28,36},{32,... | collective-permute-start | bytes 98312 | tf_op jit(solution)/shard_map/ppermute | solution.py:477
  56.3 2.3 %list.1 = (f32[11008,128]{1,0:T(8,128)S(1)}, f32[24,512]{1,0:T(8,128)S(1)}, s32[2,128]{1,0:T(2,128)S(1)}, bf16[4,512,768]{2,1,0:T(8,128)(2,1)S(1)}, f32[4,256,512]{2,1,0:T(8,128)S(1)}) custom-call(f32[128,512]{1,0:T(8,128)S(1)} %get-tuple-element.17.table, f32[4,4,512]{2,1,0:T(4,128)S(1)} %bitcast_reduce_fusion.after.quad), custom_call_target="tpu_custom_call" | custom-call | tf_op jit(solution)/shard_map/list/pallas_call | solution.py:404
  58.6 3.3 %collective-permute-done.edge = f32[4,4,512]{2,1,0:T(4,128)S(1)} collective-permute-done((f32[4,4,512]{2,1,0:T(4,128)S(1)}, f32[4,4,512]{2,1,0:T(4,128)S(1)}, u32[]{:S(2)}, u32[]{:S(2)}) %collective-permute-start) | collective-permute-done | bytes 32800 | tf_op jit(solution)/shard_map/ppermute | solution.py:477
  61.8 2.7 %deposit.1 = (f32[512,512]{1,0:T(8,128)S(1)}, f32[16,128]{1,0:T(8,128)S(1)}) custom-call(s32[2,128]{1,0:T(2,128)S(1)} %get-tuple-element.19.units, f32[11008,128]{1,0:T(8,128)S(1)} %get-tuple-element.20.codes, f32[24,512]{1,0:T(8,128)S(1)} %get-tuple-element.21.place, bf16[4,512,768]{2,1,0:T(8,128)(2,1)S(1)} %get-tuple-element.22.planes, ...), custom_call_target="tpu_custom_call" | custom-call | tf_op jit(solution)/shard_map/deposit/pallas_call | solution.py:404
  64.6 11.2 %all_to_all.28 = f32[16,1,128]{2,1,0:T(1,128)S(1)} all-to-all(f32[16,1,128]{2,1,0:T(1,128)S(1)} %bitcast.18), channel_id=1, replica_groups=mesh['y'=8,'zh'=4,'zl'=2,'c'=2,'walk'=4] {'zh','zl','c'}, dimensions={0} | all-to-all | bytes 16384 | tf_op jit(solution)/shard_map/all_to_all | solution.py:424
  75.8 11.6 %all_to_all.29 = f32[32,1,128]{2,1,0:T(1,128)S(1)} all-to-all(f32[32,1,128]{2,1,0:T(1,128)S(1)} %broadcast_in_dim.12), channel_id=1, replica_groups=mesh['y'=8,'zh'=4,'zl'=2,'c'=2,'walk'=4] {'y','walk'}, dimensions={0} | all-to-all | bytes 32768 | tf_op jit(solution)/shard_map/all_to_all | solution.py:424
  87.4 1.4 %free.1 = (f32[512,512]{1,0:T(8,128)}, f32[512,512]{1,0:T(8,128)}) custom-call(f32[32,128]{1,0:T(8,128)S(1)} %bitcast.16, f32[512,512]{1,0:T(8,128)S(1)} %get-tuple-element.25.bias), custom_call_target="tpu_custom_call" | custom-call | tf_op jit(solution)/shard_map/free/pallas_call | solution.py:404
  (4 shorter events, 0.1 us)
Async XLA Ops:
  53.8 8.0 %collective-permute-start = (f32[4,4,512]{2,1,0:T(4,128)S(1)}, f32[4,4,512]{2,1,0:T(4,128)S(1)}, u32[]{:S(2)}, u32[]{:S(2)}) collective-permute-start(f32[4,4,512]{2,1,0:T(4,128)S(1)} %bitcast_reduce_fusion.after.quad), channel_id=1, source_target_pairs={{0,504},{4,508},{8,16},{12,20},{16,8},{20,12},{24,32},{28,36},{32,... | collective-permute-start | bytes 98312 | tf_op jit(solution)/shard_map/ppermute | solution.py:477
